TPU v7x, 32 devices: a whole 2x2x4 slice. The times are simulated.
32 devices in a mesh: dp: 2 (over x), expert: 16 (over z, y, core).
Axes of the slice: x: 2, y: 2, z: 4, core: 2. Of those that a mesh axis runs over, the one named last changes fastest.
Arguments:
- queries: bfloat16 [1024, 4, 3072], P('expert', 'dp'), may hold values from -256 to 256
- key_nope: bfloat16 [1024, 4, 2048], P('expert', 'dp'), may hold values from -4 to 4
- key_rope: bfloat16 [1024, 4, 64], P('expert', 'dp'), may hold values from -4 to 4
- values: bfloat16 [1024, 4, 2048], P('expert', 'dp'), may hold values from -6 to 6
- residual: bfloat16 [1024, 4, 2048], P('expert', 'dp'), may hold values from -6 to 6
- segments: int32 [4, 1024], P('dp'), may hold values from 0 to 1, never falling along the last dimension, each value on 1 to 768 neighbouring positions
- out_proj: bfloat16 [2048, 2048], P(('dp', 'expert')), may hold values from -0.125 to 0.125
- norm_gain: bfloat16 [2048], replicated, may hold values from 0.5 to 1.5
- expert_gate: bfloat16 [16, 2048, 704], P('expert'), may hold values from -0.125 to 0.125
- expert_up: bfloat16 [16, 2048, 704], P('expert'), may hold values from -0.125 to 0.125
- expert_down: bfloat16 [16, 704, 2048], P('expert'), may hold values from -0.21875 to 0.21875
- routes: int32 [2, 16, 128, 6], P('dp', 'expert'), may hold values from 0 to 15, all different within a row; in each aligned block of 128 rows (0 to 127, 128 to 255, ..., all dimensions but the last counted through in order) at most 72 rows name the same one
- route_weights: float32 [2, 16, 128, 6], P('dp', 'expert'), may hold values from 0.1 to 0.6
Outputs:
- layer_out: bfloat16 [1024, 4, 2048], P('expert', 'dp')
Inputs may be any that keep to these rules, and one draw needn't show every extreme that they name: `routes`: each row names 6 different experts; within the rows of one device no expert is named more than 72 times.
All inputs are finite; a program needn't handle non-finite values.
Results may differ from a plain program's by a relative error of at most 0.0049.
Values may be sent and summed in bfloat16 or wider, within the bound.
A program may use at most 128 MiB of HBM per device.

v0:
```python
import jax
import jax.numpy as jnp
from jax import lax
from jax.sharding import PartitionSpec as P

HEADS = 16
NOPE = 128
ROPE = 64
V_DIM = 128
TOP = 6


EPSILON = 1e-06
QUERY_BLOCK = 512


def feed_forward(rows, gate_matrix, up_matrix, down_matrix):
    gate_part = jnp.dot(rows, gate_matrix, preferred_element_type=jnp.float32)
    up_part = jnp.dot(rows, up_matrix, preferred_element_type=jnp.float32)
    activated = (jax.nn.silu(gate_part) * up_part).astype(jnp.bfloat16)
    return jnp.dot(activated, down_matrix, preferred_element_type=jnp.float32).astype(jnp.bfloat16)


def attend_items(query_items, key_items, value_items, segment_items):
    length, count_items, qk_width = query_items.shape
    block_rows = QUERY_BLOCK
    score_scale = qk_width ** (-0.5)
    key_positions = jnp.arange(length, dtype=jnp.int32)

    def one_block(block_index):
        first_row = block_index * block_rows
        query_block = lax.dynamic_slice_in_dim(query_items, first_row, block_rows, 0)
        scores = (
            jnp.einsum("qid,kid->iqk", query_block, key_items, preferred_element_type=jnp.float32)
            * score_scale
        )
        row_positions = first_row + jnp.arange(block_rows, dtype=jnp.int32)
        row_segments = lax.dynamic_slice_in_dim(segment_items, first_row, block_rows, 1)
        allowed = (row_positions[None, :, None] >= key_positions[None, None, :]) & (
            row_segments[:, :, None] == segment_items[:, None, :]
        )
        scores = jnp.where(allowed, scores, -jnp.inf)
        row_peak = jnp.max(scores, axis=2, keepdims=True)
        raised = jnp.exp(scores - row_peak)
        weights = (raised / jnp.sum(raised, axis=2, keepdims=True)).astype(jnp.bfloat16)
        return jnp.einsum(
            "iqk,kid->qid", weights, value_items, preferred_element_type=jnp.float32
        ).astype(jnp.bfloat16)

    blocks = lax.map(one_block, jnp.arange(length // block_rows, dtype=jnp.int32))
    return blocks.reshape(length, count_items, value_items.shape[2])


def body(
    queries,
    key_nope,
    key_rope,
    values,
    residual,
    segments,
    out_proj,
    norm_gain,
    expert_gate,
    expert_up,
    expert_down,
    routes,
    route_weights,
):
    half_rows, stream_count, query_width = queries.shape
    model_width = residual.shape[2]
    token_rows = half_rows * stream_count
    expert_count = lax.axis_size("expert")
    item_count = stream_count * HEADS // expert_count
    key_heads = jnp.concatenate(
        [
            key_nope.reshape(half_rows, stream_count, HEADS, NOPE),
            jnp.broadcast_to(key_rope[:, :, None, :], (half_rows, stream_count, HEADS, ROPE)),
        ],
        axis=3,
    )
    query_items = queries.reshape(half_rows, stream_count * HEADS, NOPE + ROPE)
    key_items = key_heads.reshape(half_rows, stream_count * HEADS, NOPE + ROPE)
    value_items = values.reshape(half_rows, stream_count * HEADS, V_DIM)
    packed = jnp.concatenate([query_items, key_items, value_items], axis=2)
    packed_all = lax.all_to_all(packed, "expert", split_axis=1, concat_axis=0, tiled=True)
    qk_width = NOPE + ROPE
    query_all = packed_all[:, :, :qk_width]
    key_all = packed_all[:, :, qk_width : 2 * qk_width]
    value_all = packed_all[:, :, 2 * qk_width :]
    item_ids = lax.axis_index("expert") * item_count + jnp.arange(item_count, dtype=jnp.int32)
    stream_ids = item_ids // HEADS
    selector = (stream_ids[:, None] == jnp.arange(stream_count, dtype=jnp.int32)[None, :]).astype(
        jnp.int32
    )
    segment_items = jnp.sum(selector[:, :, None] * segments[None, :, :], axis=1)
    attended_items = attend_items(query_all, key_all, value_all, segment_items)
    attended_back = lax.all_to_all(
        attended_items, "expert", split_axis=0, concat_axis=1, tiled=True
    )
    attn_rows = attended_back.reshape(token_rows, HEADS * V_DIM)
    projected = jnp.dot(
        attn_rows,
        lax.all_gather(out_proj, ("dp", "expert"), axis=0, tiled=True),
        preferred_element_type=jnp.float32,
    )
    hidden = residual.reshape(token_rows, model_width).astype(jnp.float32) + projected
    mean_square = jnp.mean(hidden * hidden, axis=1, keepdims=True)
    normed = (hidden * lax.rsqrt(mean_square + EPSILON) * norm_gain.astype(jnp.float32)).astype(
        jnp.bfloat16
    )
    token_routes = routes.reshape(token_rows, TOP)
    token_weights = route_weights.reshape(token_rows, TOP)
    expert_ids = jnp.arange(expert_count, dtype=jnp.int32)
    weight_table = jnp.sum(
        jnp.where(
            token_routes[:, :, None] == expert_ids[None, None, :], token_weights[:, :, None], 0.0
        ),
        axis=1,
    )
    own_weights = lax.all_to_all(
        weight_table.T, "expert", split_axis=0, concat_axis=0, tiled=True
    ).reshape(expert_count * token_rows, 1)
    all_rows = lax.all_gather(normed, "expert", axis=0, tiled=True)
    results = feed_forward(all_rows, expert_gate[0], expert_up[0], expert_down[0])
    partial = (own_weights * results.astype(jnp.float32)).astype(jnp.bfloat16)
    routed_sum = lax.psum_scatter(partial, "expert", scatter_dimension=0, tiled=True).astype(
        jnp.float32
    )
    layer_out = (hidden + routed_sum).astype(jnp.bfloat16)
    return layer_out.reshape(half_rows, stream_count, model_width)


def solution(mesh):
    return jax.shard_map(
        body,
        mesh=mesh,
        in_specs=(
            P("expert", "dp", None),
            P("expert", "dp", None),
            P("expert", "dp", None),
            P("expert", "dp", None),
            P("expert", "dp", None),
            P("dp", None),
            P(("dp", "expert"), None),
            P(),
            P("expert", None, None),
            P("expert", None, None),
            P("expert", None, None),
            P("dp", "expert", None, None),
            P("dp", "expert", None, None),
        ),
        out_specs=P("expert", "dp", None),
        check_vma=False,
    )
```

profile of v0, /device:TPU:0, one launch (start us, length us, event | category | flops | bytes accessed | tf_op | source)
XLA Modules:
  0.0 368.7 jit_solution(16505499068747133357)
XLA Ops:
  7.3 1.5 concatenate.10
  8.8 2.2 reshape.126
  10.9 3.4 reshape.125
  14.4 2.3 pad_maximum_fusion
  16.7 2.5 copy.42
  19.2 7.5 %all-to-all-start = ((bf16[64,32,512]{2,0,1:T(8,128)(2,1)}), bf16[64,32,512]{2,0,1:T(8,128)(2,1)}, u32[]{:S(2)}, u32[]{:S(2)}) async-start(bf16[64,32,512]{2,0,1:T(8,128)(2,1)} %copy.42), calls=%async_computation | async-start | bytes 4194304 | tf_op jit(solution)/shard_map/all_to_all | solution.py:85
  26.9 54.6 %all-to-all-done = bf16[64,32,512]{2,0,1:T(8,128)(2,1)} async-done(((bf16[64,32,512]{2,0,1:T(8,128)(2,1)}), bf16[64,32,512]{2,0,1:T(8,128)(2,1)}, u32[]{:S(2)}, u32[]{:S(2)}) %all-to-all-start) | async-done | bytes 2097184 | tf_op jit(solution)/shard_map/all_to_all | solution.py:85
  81.5 1.8 copy.43
  84.2 1.8 fusion.47
  86.0 2.2 copy.45
  88.1 2.2 copy.44
  90.3 20.0 %while.11 = (s32[]{:T(128)}, bf16[2,512,2,128]{3,1,0,2:T(8,128)(2,1)}, s32[2]{0:T(128)S(1)}, s32[2,1024]{1,0:T(2,128)S(1)}, bf16[1024,2,192]{0,2,1:T(8,128)(2,1)...) while((s32[]{:T(128)}, ...), condition=%wide.region_4.5_spmd.clone, body=%wide.region_1.4_spmd.clone.sunk | while | flops 1088032256 | bytes 4763843 | solution.py:50
  92.0 3.4 fusion.67
  95.4 5.0 %fusion.68 = bf16[2,512,2,128]{3,1,0,2:T(8,128)(2,1)} fusion(bf16[2,512,2,128]{3,1,0,2:T(8,128)(2,1)} %get-tuple-element.172, s32[]{:T(128)S(6)} %copy.63, bf16[1024,2,128]{2,0,1:T(8,128)(2,1)} %get-tuple-element.188, f32[2,512]{1,0:T(2,128)S(1)} %fusion.67, s32[2,1024]{1,0:T(2,128)S(1)} %get-tuple-element.185, ...), kind=kOutput, calls=%fused_computation.15.clone.1 | convolution fusion | flops 678561792 | bytes 2506760 | tf_op jit(solution)/shard_map/while/body/eval_jaxpr/iqk,kid->qid/dot_general | solution.py:46
  101.9 3.4 fusion.67
  105.4 5.0 %fusion.68 = bf16[2,512,2,128]{3,1,0,2:T(8,128)(2,1)} fusion(bf16[2,512,2,128]{3,1,0,2:T(8,128)(2,1)} %get-tuple-element.172, s32[]{:T(128)S(6)} %copy.63, bf16[1024,2,128]{2,0,1:T(8,128)(2,1)} %get-tuple-element.188, f32[2,512]{1,0:T(2,128)S(1)} %fusion.67, s32[2,1024]{1,0:T(2,128)S(1)} %get-tuple-element.185, ...), kind=kOutput, calls=%fused_computation.15.clone.1 | convolution fusion | flops 678561792 | bytes 2506760 | tf_op jit(solution)/shard_map/while/body/eval_jaxpr/iqk,kid->qid/dot_general | solution.py:46
  110.3 2.4 copy.47
  112.7 16.8 %all-to-all-start.1 = ((bf16[1024,2,128]{2,1,0:T(2,128)(2,1)}), bf16[1024,2,128]{2,1,0:T(2,128)(2,1)S(1)}, u32[]{:S(2)}, u32[]{:S(2)}) async-start(bf16[1024,2,128]{2,1,0:T(2,128)(2,1)} %copy.47), calls=%async_computation.1 | async-start | bytes 1048576 | tf_op jit(solution)/shard_map/all_to_all | solution.py:97
  129.5 2.2 reshape.130
  131.8 12.0 %all-to-all-done.1 = bf16[1024,2,128]{2,1,0:T(2,128)(2,1)S(1)} async-done(((bf16[1024,2,128]{2,1,0:T(2,128)(2,1)}), bf16[1024,2,128]{2,1,0:T(2,128)(2,1)S(1)}, u32[]{:S(2)}, u32[]{:S(2)}) %all-to-all-start.1) | async-done | bytes 524320 | tf_op jit(solution)/shard_map/all_to_all | solution.py:97
  143.7 1.2 copy.57
  144.9 1.4 reshape.128
  146.4 5.0 %multiply_reduce_fusion = (f32[128]{0:T(128)S(1)}, f32[128,2048]{1,0:T(8,128)S(1)}) fusion(f32[128,2048]{1,0:T(8,128)} %reshape.130, bf16[128,2048]{1,0:T(8,128)(2,1)S(1)} %reshape.128, bf16[2048,2048]{1,0:T(8,128)(2,1)} %all-gather.3.cloned.1.call-done), kind=kOutput, calls=%fused_computation.40 | convolution fusion | flops 1074528128 | bytes 11010560 | tf_op jit(solution)/shard_map/dot_general | solution.py:101
  151.4 1.0 copy-done.1
  152.4 1.0 multiply_convert_fusion.2
  154.0 4.2 %all-to-all-start.2 = ((f32[16,1,128]{2,1,0:T(1,128)}), f32[16,1,128]{2,1,0:T(1,128)S(1)}, u32[]{:S(2)}, u32[]{:S(2)}) async-start(f32[16,1,128]{2,1,0:T(1,128)} %bitcast.9), calls=%async_computation.2 | async-start | bytes 16384 | tf_op jit(solution)/shard_map/all_to_all | solution.py:120
  158.4 68.7 %all-gather.5.cloned.1.call-done = bf16[2048,2048]{1,0:T(8,128)(2,1)} async-done(((bf16[128,2048]{1,0:T(8,128)(2,1)}), bf16[2048,2048]{1,0:T(8,128)(2,1)}) %all-gather.5.cloned.1.call-update) | async-done | bytes 8388624 | tf_op jit(solution)/shard_map/all_gather | solution.py:123
  227.2 11.1 %fusion.40 = f32[2048,704]{0,1:T(8,128)} fusion(bf16[2048,2048]{1,0:T(8,128)(2,1)} %all-gather.5.cloned.1.call-done, bf16[1,2048,704]{1,2,0:T(8,128)(2,1)} %param.23), kind=kOutput, calls=%fused_computation.33 | convolution fusion | flops 5905580032 | bytes 17039360 | tf_op jit(solution)/shard_map/dot_general | solution.py:18
  238.3 19.1 %multiply_convert_fusion = bf16[2048,2048]{1,0:T(8,128)(2,1)} fusion(f32[2048]{0:T(1024)S(1)} %bitcast.66, f32[2048,704]{0,1:T(8,128)} %fusion.40, bf16[2048,2048]{1,0:T(8,128)(2,1)} %all-gather.5.cloned.1.call-done, bf16[1,704,2048]{2,1,0:T(8,128)(2,1)S(1)} %copy-done, bf16[1,2048,704]{1,2,0:T(8,128)(2,1)} %param.24), kind=kOutput, calls=%fused_computation.29 | convolution fusion | flops 11836588032 | bytes 28319744 | tf_op jit(solution)/shard_map/dot_general | solution.py:21
  257.4 102.2 %reduce-scatter.2.cloned.1.call-done = bf16[128,2048]{1,0:T(8,128)(2,1)} async-done(((bf16[2048,2048]{1,0:T(8,128)(2,1)}), bf16[128,2048]{1,0:T(8,128)(2,1)}) %reduce-scatter.2.cloned.1.call-update) | async-done | bytes 524304 | tf_op jit(solution)/shard_map/reduce_scatter | solution.py:126
  359.6 1.5 add_convert_fusion
  361.0 1.1 reshape.129
  (41 shorter events, 4.8 us)
Async XLA Ops:
  6.5 231.8 %copy-start = (bf16[1,704,2048]{2,1,0:T(8,128)(2,1)S(1)}, bf16[1,704,2048]{2,1,0:T(8,128)(2,1)}, u32[]{:S(2)}) copy-start(bf16[1,704,2048]{2,1,0:T(8,128)(2,1)} %param.25) | copy-start | bytes 8650756
  6.5 7.8 %copy-start.2 = (bf16[64,2,64]{2,1,0:T(2,128)(2,1)S(1)}, bf16[64,2,64]{2,1,0:T(2,128)(2,1)}, u32[]{:S(2)}) copy-start(bf16[64,2,64]{2,1,0:T(2,128)(2,1)} %param.17) | copy-start | bytes 49156
  6.5 139.8 %all-gather.3.cloned.1.call-start = ((), (), s32[]{:S(2)}) async-start(), calls=%async_computation.4 | async-start | bytes 8650752 | tf_op jit(solution)/shard_map/all_gather | solution.py:103
  16.7 10.1 %copy-start.3 = (s32[2,1024]{1,0:T(2,128)S(1)}, s32[2,1024]{1,0:T(2,128)}, u32[]{:S(2)}) copy-start(s32[2,1024]{1,0:T(2,128)} %param.20) | copy-start | bytes 24580
  19.2 62.3 %all-to-all-start = ((bf16[64,32,512]{2,0,1:T(8,128)(2,1)}), bf16[64,32,512]{2,0,1:T(8,128)(2,1)}, u32[]{:S(2)}, u32[]{:S(2)}) async-start(bf16[64,32,512]{2,0,1:T(8,128)(2,1)} %copy.42), calls=%async_computation | async-start | bytes 4194304 | tf_op jit(solution)/shard_map/all_to_all | solution.py:85
  90.3 39.2 %copy-start.4 = (bf16[2048]{0:T(1024)(128)(2,1)S(1)}, bf16[2048]{0:T(1024)(128)(2,1)}, u32[]{:S(2)}) copy-start(bf16[2048]{0:T(1024)(128)(2,1)} %param.22) | copy-start | bytes 12292
  112.7 31.0 %all-to-all-start.1 = ((bf16[1024,2,128]{2,1,0:T(2,128)(2,1)}), bf16[1024,2,128]{2,1,0:T(2,128)(2,1)S(1)}, u32[]{:S(2)}, u32[]{:S(2)}) async-start(bf16[1024,2,128]{2,1,0:T(2,128)(2,1)} %copy.47), calls=%async_computation.1 | async-start | bytes 1048576 | tf_op jit(solution)/shard_map/all_to_all | solution.py:97
  129.5 97.7 %all-gather.5.cloned.1.call-start = ((), (), s32[]{:S(2)}) async-start(), calls=%async_computation.5 | async-start | bytes 8912896 | tf_op jit(solution)/shard_map/all_gather | solution.py:123
  146.3 7.0 %copy-start.5 = (s32[1,1,128,6]{2,1,3,0:T(1,128)S(1)}, s32[1,1,128,6]{2,1,3,0:T(1,128)}, u32[]{:S(2)}) copy-start(s32[1,1,128,6]{2,1,3,0:T(1,128)} %param.26) | copy-start | bytes 9220
  146.3 7.0 %copy-start.6 = (f32[1,1,128,6]{2,1,3,0:T(1,128)S(1)}, f32[1,1,128,6]{2,1,3,0:T(1,128)}, u32[]{:S(2)}) copy-start(f32[1,1,128,6]{2,1,3,0:T(1,128)} %param.27) | copy-start | bytes 9220
  151.3 1.0 copy-start.1
  154.0 84.3 %all-to-all-start.2 = ((f32[16,1,128]{2,1,0:T(1,128)}), f32[16,1,128]{2,1,0:T(1,128)S(1)}, u32[]{:S(2)}, u32[]{:S(2)}) async-start(f32[16,1,128]{2,1,0:T(1,128)} %bitcast.9), calls=%async_computation.2 | async-start | bytes 16384 | tf_op jit(solution)/shard_map/all_to_all | solution.py:120
  158.2 201.4 %reduce-scatter.2.cloned.1.call-start = ((), (), s32[]{:S(2)}) async-start(), calls=%async_computation.6 | async-start | bytes 8912896 | tf_op jit(solution)/shard_map/reduce_scatter | solution.py:126
Sparse Core Ops, SparseCore 0:
  10.2 105.4 all-gather.2
  153.5 73.6 all-gather.4
  257.5 102.0 reduce-scatter.1
where the time goes:
time: 369 us
  waiting for transfers between devices  238 us (64%)
  matrix products  51.9 us (14%)
  local copies, waits for them, and re-layouts  29 us (8%)
  starting transfers between devices  28.7 us (8%)
  between operations  13.3 us (4%)
  other arithmetic  6.22 us (2%)
    reduce_scatter x1, waiting for transfers between devices, body(): lax.psum_scatter(partial, 'expert', scatter_dimension=0, tiled=True)  102 us
    all_gather x1, waiting for transfers between devices, body(): all_rows = lax.all_gather(normed, 'expert', axis=0, tiled=True)  68.7 us
    all_to_all x1, waiting for transfers between devices, body(): lax.all_to_all(packed, 'expert', split_axis=1, concat_axis=0, tiled=True)  54.6 us
    dot_general x1, matrix products, feed_forward(): jnp.dot(activated, down_matrix, preferred_element_type=jnp.float32)  19.1 us
    all_to_all x1, starting transfers between devices, body(): lax.all_to_all(attended_items, 'expert', split_axis=0, concat_axis=1, til...  16.8 us
    all_to_all x1, waiting for transfers between devices, body(): lax.all_to_all(attended_items, 'expert', split_axis=0, concat_axis=1, til...  12 us
    dot_general x1, matrix products, feed_forward(): gate_part = jnp.dot(rows, gate_matrix, preferred_element_type=jnp.float32)  11.1 us
    dot_general x2, matrix products, one_block(): jnp.einsum('iqk,kid->qid', weights, value_items, preferred_element_type=j...  9.9 us
  transfers between devices with their start and end apart: 6, of which 4 were waited for; matrix products, arithmetic and copies ran while one was open for 16% of the time, Pallas kernels for 0%

commit v1 on v0

--- a/solution.py
+++ b/solution.py
@@ -1,6 +1,10 @@
+import functools
+
 import jax
 import jax.numpy as jnp
 from jax import lax
+from jax.experimental import pallas as pl
+from jax.experimental.pallas import tpu as pltpu
 from jax.sharding import PartitionSpec as P
 
 HEADS = 16
@@ -14,11 +18,307 @@
 QUERY_BLOCK = 512
 
 
-def feed_forward(rows, gate_matrix, up_matrix, down_matrix):
-    gate_part = jnp.dot(rows, gate_matrix, preferred_element_type=jnp.float32)
-    up_part = jnp.dot(rows, up_matrix, preferred_element_type=jnp.float32)
-    activated = (jax.nn.silu(gate_part) * up_part).astype(jnp.bfloat16)
-    return jnp.dot(activated, down_matrix, preferred_element_type=jnp.float32).astype(jnp.bfloat16)
+MESH = pl.DeviceIdType.MESH
+
+
+def ring_position(chip, chips):
+    odd = chip % 2
+    return (1 - odd) * (chip // 2) + odd * (chips - 1 - chip // 2)
+
+
+def ring_chip(position, chips):
+    back = position // (chips // 2)
+    return (1 - back) * (2 * position) + back * (2 * (chips - 1 - position) + 1)
+
+
+def expert_kernel(
+    chips,
+    x_ref,
+    table_ref,
+    hidden_ref,
+    gate_ref,
+    up_ref,
+    down_ref,
+    out_ref,
+    rows_all,
+    table_all,
+    own_part,
+    mate_part,
+    ring_in,
+    act,
+    gate_vmem,
+    up_vmem,
+    down_vmem,
+    weight_sem,
+    x_send,
+    x_recv,
+    t_send,
+    t_recv,
+    m_send,
+    m_recv,
+    r_send,
+    r_recv,
+):
+    tokens, width = x_ref.shape
+    half = tokens // 2
+    far = chips // 2
+    me = lax.axis_index("expert")
+    core = me % 2
+    position = ring_position(me // 2, chips)
+    after = 2 * ring_chip((position + 1) % chips, chips) + core
+    before = 2 * ring_chip((position + chips - 1) % chips, chips) + core
+    mate = me + 1 - 2 * core
+    def slot_of(way, distance):
+        if distance == 0:
+            return 0
+        if distance == far:
+            return chips - 1
+        return 2 * distance - 1 + way
+
+    def reach(way, part):
+        return far if part == way else far - 1
+
+    targets = (after, before)
+
+    barrier = pltpu.get_barrier_semaphore()
+    for other in (after, before, mate):
+        pl.semaphore_signal(barrier, inc=1, device_id={"expert": other}, device_id_type=MESH)
+
+    loads = [
+        pltpu.make_async_copy(src, dst, weight_sem.at[i])
+        for i, (src, dst) in enumerate(
+            ((gate_ref, gate_vmem), (up_ref, up_vmem), (down_ref, down_vmem))
+        )
+    ]
+    for load in loads:
+        load.start()
+    pl.semaphore_wait(barrier, 3)
+
+    def remote(src, dst, send, recv, other):
+        return pltpu.make_async_remote_copy(
+            src_ref=src,
+            dst_ref=dst,
+            send_sem=send,
+            recv_sem=recv,
+            device_id={"expert": other},
+            device_id_type=MESH,
+        )
+
+    def rows_of(part):
+        return pl.ds(part * half, half)
+
+    def row_copy(way, distance, part):
+        if way == 2:
+            slot = distance
+            src = x_ref.at[rows_of(part)] if slot == 0 else rows_all.at[slot, 0, rows_of(part)]
+            dst = rows_all.at[slot, 1, rows_of(part)]
+            other = mate
+        else:
+            slot = slot_of(way, distance)
+            src = (
+                x_ref.at[rows_of(part)]
+                if distance == 1
+                else rows_all.at[slot_of(way, distance - 1), 0, rows_of(part)]
+            )
+            dst = rows_all.at[slot, 0, rows_of(part)]
+            other = targets[way]
+        return remote(
+            src, dst, x_send.at[way, distance, part], x_recv.at[way, distance, part], other
+        )
+
+    def table_copy(way, distance):
+        if way == 2:
+            slot = distance
+            src = table_ref if slot == 0 else table_all.at[slot, 0]
+            dst = table_all.at[slot, 1]
+            other = mate
+        else:
+            slot = slot_of(way, distance)
+            src = table_ref if distance == 1 else table_all.at[slot_of(way, distance - 1), 0]
+            dst = table_all.at[slot, 0]
+            other = targets[way]
+        return remote(src, dst, t_send.at[way, distance], t_recv.at[way, distance], other)
+
+    sent = []
+
+    def start(copy):
+        copy.start()
+        sent.append(copy)
+
+    def table_goes(way, distance):
+        return distance < far or way == 0
+
+    for part in range(2):
+        for way in range(2):
+            start(row_copy(way, 1, (part + way) % 2))
+        start(row_copy(2, 0, part))
+    for way in range(2):
+        start(table_copy(way, 1))
+    start(table_copy(2, 0))
+
+    def serve(distance, turn):
+        for way in range(2):
+            part = (turn + way) % 2
+            if distance > reach(way, part):
+                continue
+            row_copy(way, distance, part).wait_recv()
+            if distance + 1 <= reach(way, part):
+                start(row_copy(way, distance + 1, part))
+            start(row_copy(2, slot_of(way, distance), part))
+            if turn == 0 and table_goes(way, distance):
+                table_copy(way, distance).wait_recv()
+                if distance + 1 <= far and table_goes(way, distance + 1):
+                    start(table_copy(way, distance + 1))
+                start(table_copy(2, slot_of(way, distance)))
+
+    def mate_copy(slot):
+        return remote(
+            rows_all.at[slot, 1], mate_part.at[slot], m_send.at[slot], m_recv.at[slot], mate
+        )
+
+    hidden_units = gate_vmem.shape[0]
+    eye = lax.broadcasted_iota(jnp.int32, (tokens, tokens), 0) == lax.broadcasted_iota(
+        jnp.int32, (tokens, tokens), 1
+    )
+
+    def column(row):
+        return jnp.sum(jnp.where(eye, row, 0.0), axis=1, keepdims=True)
+
+    def experts(slot):
+        for part in range(2):
+            row_copy(2, slot, part).wait_recv()
+        table_copy(2, slot).wait_recv()
+        mine = x_ref[...] if slot == 0 else rows_all[slot, 0]
+        rows = jnp.concatenate([mine, rows_all[slot, 1]], axis=0)
+        for first in range(0, hidden_units, 256):
+            count = min(256, hidden_units - first)
+            dims = (((1,), (1,)), ((), ()))
+            gate_part = lax.dot_general(
+                rows, gate_vmem[first : first + count, :], dims, preferred_element_type=jnp.float32
+            )
+            up_part = lax.dot_general(
+                rows, up_vmem[first : first + count, :], dims, preferred_element_type=jnp.float32
+            )
+            silu = gate_part / (1.0 + jnp.exp(-gate_part))
+            act[:, first : first + count] = (silu * up_part).astype(jnp.bfloat16)
+        own_table = table_ref if slot == 0 else table_all.at[slot, 0]
+        own_column = column(own_table[pl.ds(me, 1), :])
+        mate_column = column(table_all[slot, 1, pl.ds(me, 1), :])
+        for first in range(0, width, 512):
+            y = jnp.dot(
+                act[...], down_vmem[:, first : first + 512], preferred_element_type=jnp.float32
+            )
+            own_part[slot, :, first : first + 512] = (y[:tokens] * own_column).astype(jnp.bfloat16)
+            rows_all[slot, 1, :, first : first + 512] = (y[tokens:] * mate_column).astype(
+                jnp.bfloat16
+            )
+        start(mate_copy(slot))
+
+    def sum_slot(way, distance):
+        return slot_of(1 - way, distance)
+
+    def sum_copy(way, distance, part):
+        return remote(
+            own_part.at[sum_slot(way, distance), rows_of(part)],
+            ring_in.at[way, distance - 1, part],
+            r_send.at[way, distance, part],
+            r_recv.at[way, distance, part],
+            targets[way],
+        )
+
+    mated = set()
+
+    def mated_wait(slot):
+        if slot not in mated:
+            mated.add(slot)
+            mate_copy(slot).wait_recv()
+
+    def chip_sum(slot, part):
+        mated_wait(slot)
+        return own_part[slot, rows_of(part), :].astype(jnp.float32) + mate_part[
+            slot, rows_of(part), :
+        ].astype(jnp.float32)
+
+    def send_sum(distance, late):
+        for way in range(2):
+            part = way if late else 1 - way
+            if distance > reach(way, part):
+                continue
+            slot = sum_slot(way, distance)
+            total = chip_sum(slot, part)
+            if distance < reach(way, part):
+                sum_copy(way, distance + 1, part).wait_recv()
+                total = total + ring_in[way, distance, part].astype(jnp.float32)
+            own_part[slot, rows_of(part), :] = total.astype(jnp.bfloat16)
+            start(sum_copy(way, distance, part))
+
+    for load in loads:
+        load.wait()
+    experts(0)
+    serve(1, 0)
+    serve(1, 1)
+    for distance in range(1, far):
+        experts(slot_of(0, distance))
+        serve(distance + 1, 0)
+        experts(slot_of(1, distance))
+        if distance + 1 < far:
+            serve(distance + 1, 1)
+    send_sum(far - 1, False)
+    experts(slot_of(0, far))
+    send_sum(far, True)
+    for distance in range(far - 2, 0, -1):
+        send_sum(distance, False)
+        send_sum(distance + 1, True)
+    send_sum(1, True)
+    for part in range(2):
+        total = hidden_ref[rows_of(part), :] + chip_sum(0, part)
+        for way in range(2):
+            sum_copy(way, 1, part).wait_recv()
+            total = total + ring_in[way, 0, part].astype(jnp.float32)
+        out_ref[rows_of(part), :] = total.astype(jnp.bfloat16)
+    for copy in sent:
+        copy.wait_send()
+
+
+def routed_experts(normed, table, hidden, gate, up, down):
+    tokens, width = normed.shape
+    count = table.shape[0]
+    chips = count // 2
+    units = gate.shape[0]
+    half = tokens // 2
+    vmem = pl.BlockSpec(memory_space=pltpu.VMEM)
+    anywhere = pl.BlockSpec(memory_space=pl.ANY)
+    dma = pltpu.SemaphoreType.DMA
+    far = chips // 2
+    return pl.pallas_call(
+        functools.partial(expert_kernel, chips),
+        out_shape=jax.ShapeDtypeStruct((tokens, width), jnp.bfloat16),
+        in_specs=[vmem, vmem, vmem, anywhere, anywhere, anywhere],
+        out_specs=vmem,
+        scratch_shapes=[
+            pltpu.VMEM((chips, 2, tokens, width), jnp.bfloat16),
+            pltpu.VMEM((chips, 2, count, tokens), jnp.float32),
+            pltpu.VMEM((chips, tokens, width), jnp.bfloat16),
+            pltpu.VMEM((chips, tokens, width), jnp.bfloat16),
+            pltpu.VMEM((2, far, 2, half, width), jnp.bfloat16),
+            pltpu.VMEM((2 * tokens, units), jnp.bfloat16),
+            pltpu.VMEM((units, width), jnp.bfloat16),
+            pltpu.VMEM((units, width), jnp.bfloat16),
+            pltpu.VMEM((units, width), jnp.bfloat16),
+            dma((3,)),
+            dma((3, chips, 2)),
+            dma((3, chips, 2)),
+            dma((3, chips)),
+            dma((3, chips)),
+            dma((chips,)),
+            dma((chips,)),
+            dma((2, far + 1, 2)),
+            dma((2, far + 1, 2)),
+        ],
+        compiler_params=pltpu.CompilerParams(
+            collective_id=1, has_side_effects=True, vmem_limit_bytes=64000000
+        ),
+    )(normed, table, hidden, gate, up, down)
 
 
 def attend_items(query_items, key_items, value_items, segment_items):
@@ -117,16 +417,14 @@
         ),
         axis=1,
     )
-    own_weights = lax.all_to_all(
-        weight_table.T, "expert", split_axis=0, concat_axis=0, tiled=True
-    ).reshape(expert_count * token_rows, 1)
-    all_rows = lax.all_gather(normed, "expert", axis=0, tiled=True)
-    results = feed_forward(all_rows, expert_gate[0], expert_up[0], expert_down[0])
-    partial = (own_weights * results.astype(jnp.float32)).astype(jnp.bfloat16)
-    routed_sum = lax.psum_scatter(partial, "expert", scatter_dimension=0, tiled=True).astype(
-        jnp.float32
-    )
-    layer_out = (hidden + routed_sum).astype(jnp.bfloat16)
+    layer_out = routed_experts(
+        normed,
+        weight_table.T,
+        hidden,
+        jnp.swapaxes(expert_gate[0], 0, 1),
+        jnp.swapaxes(expert_up[0], 0, 1),
+        expert_down[0],
+    )
     return layer_out.reshape(half_rows, stream_count, model_width)
 
 

time: 369 us -> 238 us (0.64)
  waiting for transfers between devices: 238 us -> 69.9 us
  Pallas kernels: 0 us -> 96.5 us
  matrix products: 51.9 us -> 16.1 us
  local copies, waits for them, and re-layouts: 29 us -> 17.4 us
  starting transfers between devices: 28.7 us -> 18.7 us
    reduce_scatter x1 -> x0, waiting for transfers between devices: 102 us -> none  [body(): lax.psum_scatter(partial, 'expert', scatter_dimension=0, tiled=True)]
    pallas_call x0 -> x1, Pallas kernels: none -> 96.5 us  [routed_experts(): pl.pallas_call(functools.partial(expert_kernel, chips), out_shape=jax.Sha...]
    all_gather x1 -> x0, waiting for transfers between devices: 68.7 us -> none  [body(): all_rows = lax.all_gather(normed, 'expert', axis=0, tiled=True)]
    dot_general x2 -> x0, matrix products: 30.2 us -> none  [the longest x1 19.1 us: feed_forward(): jnp.dot(activated, down_matrix, preferred_element_type=jnp.float32)]
    all_to_all x1, starting transfers between devices: 16.8 us -> 11.2 us  [body(): lax.all_to_all(attended_items, 'expert', split_axis=0, concat_axis=1, til...]
    unnamed x18, local copies, waits for them, and re-layouts: 5.4 us -> 1.07 us
    all_to_all x1 -> x0, starting transfers between devices: 4.16 us -> none  [body(): lax.all_to_all(weight_table.T, 'expert', split_axis=0, concat_axis=0, til...]
  transfers between devices with their start and end apart: 6 -> 3, of which waited for: 4 -> 2; matrix products, arithmetic and copies ran while one was open for 16% -> 12% of each run, Pallas kernels for 0% -> 0%
where the time goes in v1:
time: 238 us; the launch traced here: 237 us
  Pallas kernels  96.5 us (41%)
  waiting for transfers between devices  69.9 us (29%)
  starting transfers between devices  18.7 us (8%)
  local copies, waits for them, and re-layouts  17.4 us (7%)
  matrix products  16.1 us (7%)
  between operations  13.6 us (6%)
  other arithmetic  3.51 us (1%)
    pallas_call x1, Pallas kernels, routed_experts(): pl.pallas_call(functools.partial(expert_kernel, chips), out_shape=jax.Sha...  96.5 us
    all_to_all x1, waiting for transfers between devices, body(): lax.all_to_all(packed, 'expert', split_axis=1, concat_axis=0, tiled=True)  56 us
    all_to_all x1, waiting for transfers between devices, body(): lax.all_to_all(attended_items, 'expert', split_axis=0, concat_axis=1, til...  13.2 us
    all_to_all x1, starting transfers between devices, body(): lax.all_to_all(attended_items, 'expert', split_axis=0, concat_axis=1, til...  11.2 us
    all_to_all x1, starting transfers between devices, body(): lax.all_to_all(packed, 'expert', split_axis=1, concat_axis=0, tiled=True)  7.42 us
    dot_general x2, matrix products, one_block(): jnp.einsum('iqk,kid->qid', weights, value_items, preferred_element_type=j...  7.09 us
  transfers between devices with their start and end apart: 3, of which 2 were waited for; matrix products, arithmetic and copies ran while one was open for 12% of the time, Pallas kernels for 0%

profile of v1, /device:TPU:0, one launch (start us, length us, event | category | flops | bytes accessed | tf_op | source)
XLA Modules:
  0.0 237.1 jit_solution(15548099305247582764)
XLA Ops:
  6.5 0.7 all-gather.2.cloned.1.call-update
  7.3 2.6 %reshape.120 = bf16[64,32,192]{2,1,0:T(8,128)(2,1)S(1)} reshape(bf16[64,2,3072]{2,1,0:T(2,128)(2,1)} %param.15) | data formatting | bytes 1572864 | tf_op jit(solution)/shard_map/reshape | solution.py:381
  9.9 1.4 concatenate.10
  11.2 1.4 reshape.121
  12.7 0.9 pad_maximum_fusion
  13.6 2.6 %copy.42 = bf16[64,32,512]{2,0,1:T(8,128)(2,1)} copy(bf16[64,32,512]{2,1,0:T(8,128)(2,1)S(1)} %pad_maximum_fusion) | data formatting | bytes 4194304 | tf_op jit(solution)/shard_map/concatenate | solution.py:384
  16.2 7.4 %all-to-all-start = ((bf16[64,32,512]{2,0,1:T(8,128)(2,1)}), bf16[64,32,512]{2,0,1:T(8,128)(2,1)S(1)}, u32[]{:S(2)}, u32[]{:S(2)}) async-start(bf16[64,32,512]{2,0,1:T(8,128)(2,1)} %copy.42), calls=%async_computation | async-start | bytes 4194304 | tf_op jit(solution)/shard_map/all_to_all | solution.py:385
  23.8 56.0 %all-to-all-done = bf16[64,32,512]{2,0,1:T(8,128)(2,1)S(1)} async-done(((bf16[64,32,512]{2,0,1:T(8,128)(2,1)}), bf16[64,32,512]{2,0,1:T(8,128)(2,1)S(1)}, u32[]{:S(2)}, u32[]{:S(2)}) %all-to-all-start) | async-done | bytes 2097184 | tf_op jit(solution)/shard_map/all_to_all | solution.py:385
  79.8 0.2 copy.43
  80.0 0.9 slice.14
  80.9 0.5 fusion.40
  81.4 0.5 copy.44
  81.9 0.5 copy.45
  82.5 14.7 %while.11 = (s32[]{:T(128)}, bf16[2,512,2,128]{3,1,0,2:T(8,128)(2,1)}, s32[2]{0:T(128)S(1)}, s32[2,1024]{1,0:T(2,128)S(1)}, bf16[1024,2,192]{0,2,1:T(8,128)(2,1)...) while((s32[]{:T(128)}, ...), condition=%wide.region_4.5_spmd.clone, body=%wide.region_1.4_spmd.clone.sunk | while | flops 1088032256 | bytes 6861523 | solution.py:350
  82.5 0.6 dynamic_slice.34
  83.8 0.4 iota_compare_fusion.3
  84.2 2.1 fusion.58
  86.3 3.5 %fusion.59 = bf16[2,512,2,128]{3,1,0,2:T(8,128)(2,1)} fusion(bf16[2,512,2,128]{3,1,0,2:T(8,128)(2,1)} %get-tuple-element.172, s32[]{:T(128)} %get-tuple-element.171, bf16[1024,2,128]{2,0,1:T(8,128)(2,1)S(1)} %copy-done.2, f32[2,512]{1,0:T(2,128)S(1)} %fusion.58, s32[2,1024]{1,0:T(2,128)S(1)} %get-tuple-element.185, ...), kind=kOutput, calls=%fused_computation.15.clone.1 | convolution fusion | flops 678561792 | bytes 2507268 | tf_op jit(solution)/shard_map/while/body/eval_jaxpr/iqk,kid->qid/dot_general | solution.py:346
  89.8 0.6 dynamic_slice.34
  91.1 0.4 iota_compare_fusion.3
  91.5 2.1 fusion.58
  93.6 3.5 %fusion.59 = bf16[2,512,2,128]{3,1,0,2:T(8,128)(2,1)} fusion(bf16[2,512,2,128]{3,1,0,2:T(8,128)(2,1)} %get-tuple-element.172, s32[]{:T(128)} %get-tuple-element.171, bf16[1024,2,128]{2,0,1:T(8,128)(2,1)S(1)} %copy-done.2, f32[2,512]{1,0:T(2,128)S(1)} %fusion.58, s32[2,1024]{1,0:T(2,128)S(1)} %get-tuple-element.185, ...), kind=kOutput, calls=%fused_computation.15.clone.1 | convolution fusion | flops 678561792 | bytes 2507268 | tf_op jit(solution)/shard_map/while/body/eval_jaxpr/iqk,kid->qid/dot_general | solution.py:346
  97.2 2.4 %copy.47 = bf16[1024,2,128]{2,1,0:T(2,128)(2,1)} copy(bf16[1024,2,128]{2,0,1:T(8,128)(2,1)} %bitcast.57) | data formatting | bytes 1048576 | tf_op jit(solution)/shard_map/reshape | solution.py:351
  99.6 11.2 %all-to-all-start.1 = ((bf16[1024,2,128]{2,1,0:T(2,128)(2,1)}), bf16[1024,2,128]{2,1,0:T(2,128)(2,1)S(1)}, u32[]{:S(2)}, u32[]{:S(2)}) async-start(bf16[1024,2,128]{2,1,0:T(2,128)(2,1)} %copy.47), calls=%async_computation.1 | async-start | bytes 1048576 | tf_op jit(solution)/shard_map/all_to_all | solution.py:397
  111.1 0.6 select_reduce_fusion
  111.7 13.2 %all-to-all-done.1 = bf16[1024,2,128]{2,1,0:T(2,128)(2,1)S(1)} async-done(((bf16[1024,2,128]{2,1,0:T(2,128)(2,1)}), bf16[1024,2,128]{2,1,0:T(2,128)(2,1)S(1)}, u32[]{:S(2)}, u32[]{:S(2)}) %all-to-all-start.1) | async-done | bytes 524320 | tf_op jit(solution)/shard_map/all_to_all | solution.py:397
  124.9 0.4 copy.56
  125.3 0.4 reshape.123
  125.7 4.8 %multiply_reduce_fusion = (f32[128]{0:T(128)S(1)}, f32[128,2048]{1,0:T(8,128)S(1)}) fusion(f32[128,2048]{1,0:T(8,128)S(1)} %reshape.125, bf16[128,2048]{1,0:T(8,128)(2,1)S(1)} %reshape.123, bf16[2048,2048]{1,0:T(8,128)(2,1)} %all-gather.2.cloned.1.call-done), kind=kOutput, calls=%fused_computation.32 | convolution fusion | flops 1074528128 | bytes 11010560 | tf_op jit(solution)/shard_map/dot_general | solution.py:401
  130.5 1.1 multiply_convert_fusion.x_ref
  131.6 96.5 %shard_map.127 = bf16[128,2048]{1,0:T(8,128)(2,1)} custom-call(bf16[128,2048]{1,0:T(8,128)(2,1)} %multiply_convert_fusion.x_ref, f32[16,128]{1,0:T(8,128)} %bitcast.58, f32[128,2048]{1,0:T(8,128)} %copy-done, bf16[704,2048]{1,0:T(8,128)(2,1)} %bitcast.51, bf16[704,2048]{1,0:T(8,128)(2,1)} %bitcast.52, bf16[704,2048]{1,0:T(8,128)(2,1)} %bitcast.53), custom_call_target="tpu_custom_call" | custom-call | tf_op jit(solution)/shard_map/pallas_call | solution.py:293
  228.1 2.2 reshape.124
  (35 shorter events, 0.5 us)
Async XLA Ops:
  6.5 6.1 %copy-start.3 = (bf16[64,2,64]{2,1,0:T(2,128)(2,1)S(1)}, bf16[64,2,64]{2,1,0:T(2,128)(2,1)}, u32[]{:S(2)}) copy-start(bf16[64,2,64]{2,1,0:T(2,128)(2,1)} %param.17) | copy-start | bytes 49156
  6.5 119.1 %all-gather.2.cloned.1.call-start = ((), (), s32[]{:S(2)}) async-start(), calls=%async_computation.2 | async-start | bytes 8650752 | tf_op jit(solution)/shard_map/all_gather | solution.py:403
  13.6 10.1 %copy-start.4 = (s32[2,1024]{1,0:T(2,128)S(1)}, s32[2,1024]{1,0:T(2,128)}, u32[]{:S(2)}) copy-start(s32[2,1024]{1,0:T(2,128)} %param.20) | copy-start | bytes 24580
  16.2 63.6 %all-to-all-start = ((bf16[64,32,512]{2,0,1:T(8,128)(2,1)}), bf16[64,32,512]{2,0,1:T(8,128)(2,1)S(1)}, u32[]{:S(2)}, u32[]{:S(2)}) async-start(bf16[64,32,512]{2,0,1:T(8,128)(2,1)} %copy.42), calls=%async_computation | async-start | bytes 4194304 | tf_op jit(solution)/shard_map/all_to_all | solution.py:385
  82.4 28.4 %copy-start.1 = (bf16[64,2,2048]{2,1,0:T(2,128)(2,1)S(1)}, bf16[64,2,2048]{2,1,0:T(2,128)(2,1)}, u32[]{:S(2)}) copy-start(bf16[64,2,2048]{2,1,0:T(2,128)(2,1)} %param.19) | copy-start | bytes 1572868
  82.4 28.6 %copy-start.5 = (bf16[2048]{0:T(1024)(128)(2,1)S(1)}, bf16[2048]{0:T(1024)(128)(2,1)}, u32[]{:S(2)}) copy-start(bf16[2048]{0:T(1024)(128)(2,1)} %param.22) | copy-start | bytes 12292
  82.4 28.6 %copy-start.6 = (f32[1,1,128,6]{2,1,3,0:T(1,128)S(1)}, f32[1,1,128,6]{2,1,3,0:T(1,128)}, u32[]{:S(2)}) copy-start(f32[1,1,128,6]{2,1,3,0:T(1,128)} %param.27) | copy-start | bytes 9220
  82.5 28.6 %copy-start.7 = (s32[1,1,128,6]{2,1,3,0:T(1,128)S(1)}, s32[1,1,128,6]{2,1,3,0:T(1,128)}, u32[]{:S(2)}) copy-start(s32[1,1,128,6]{2,1,3,0:T(1,128)} %param.26) | copy-start | bytes 9220
  84.2 2.1 copy-start.2
  91.5 2.1 copy-start.2
  99.6 25.3 %all-to-all-start.1 = ((bf16[1024,2,128]{2,1,0:T(2,128)(2,1)}), bf16[1024,2,128]{2,1,0:T(2,128)(2,1)S(1)}, u32[]{:S(2)}, u32[]{:S(2)}) async-start(bf16[1024,2,128]{2,1,0:T(2,128)(2,1)} %copy.47), calls=%async_computation.1 | async-start | bytes 1048576 | tf_op jit(solution)/shard_map/all_to_all | solution.py:397
  130.4 1.1 copy-start
Sparse Core Ops, SparseCore 0:
  10.2 105.1 all-gather.1

commit v2 on v1

--- a/solution.py
+++ b/solution.py
@@ -321,6 +321,429 @@
     )(normed, table, hidden, gate, up, down)
 
 
+def flip(device, bit):
+    return device + bit - 2 * bit * ((device // bit) % 2)
+
+
+def attention_kernel(
+    peers,
+    q_ref,
+    nope_ref,
+    rope_ref,
+    value_ref,
+    residual_ref,
+    segments_ref,
+    proj_ref,
+    gain_ref,
+    hidden_ref,
+    normed_ref,
+    q_own,
+    q_stage,
+    mix_stage,
+    q_in,
+    mix_in,
+    nope_in,
+    value_in,
+    q_all,
+    key_all,
+    value_all,
+    out_stage,
+    attn,
+    proj,
+    load_sem,
+    a_send,
+    a_recv,
+    b_send,
+    b_recv,
+    c_send,
+    c_recv,
+):
+    block, streams, _ = q_ref.shape
+    length = block * peers
+    head = NOPE
+    width = proj_ref.shape[1]
+    proj_rows = proj_ref.shape[0]
+    me = lax.axis_index("expert")
+    plane = lax.axis_index("dp")
+    mate, row_mate = flip(me, 1), flip(me, 2)
+    near, far = flip(me, peers // 4), flip(me, peers // 2)
+
+    barrier = pltpu.get_barrier_semaphore()
+    for offset in range(1, peers):
+        pl.semaphore_signal(
+            barrier,
+            inc=1,
+            device_id={"dp": plane, "expert": (me + offset) % peers},
+            device_id_type=MESH,
+        )
+    pl.semaphore_signal(
+        barrier, inc=1, device_id={"dp": 1 - plane, "expert": me}, device_id_type=MESH
+    )
+
+    def own_columns(first):
+        return pl.ds(pl.multiple_of(first, head), head)
+
+    def own_places(device):
+        return pl.ds(pl.multiple_of(device * block, block), block)
+
+    def proj_place(part, device):
+        return pl.ds(
+            pl.multiple_of((part * peers + device) * proj_rows, proj_rows), proj_rows
+        )
+
+    load_q = pltpu.make_async_copy(q_ref, q_own, load_sem.at[0])
+    load_rope = pltpu.make_async_copy(rope_ref, mix_stage.at[0], load_sem.at[1])
+    load_proj = pltpu.make_async_copy(
+        proj_ref, proj.at[proj_place(plane, me)], load_sem.at[2]
+    )
+    for load in (load_q, load_rope, load_proj):
+        load.start()
+    pl.semaphore_wait(barrier, peers)
+
+    def remote(src, dst, send, recv, part, other):
+        return pltpu.make_async_remote_copy(
+            src_ref=src,
+            dst_ref=dst,
+            send_sem=send,
+            recv_sem=recv,
+            device_id={"dp": part, "expert": other},
+            device_id_type=MESH,
+        )
+
+    sent = []
+
+    def start(copy):
+        copy.start()
+        sent.append(copy)
+
+    partners = (
+        (plane, far),
+        (plane, near),
+        (plane, row_mate),
+        (1 - plane, me),
+        (plane, mate),
+    )
+
+    def proj_copy(stage, index, src_part, src_device, from_input=False):
+        place = proj.at[proj_place(src_part, src_device)]
+        part, other = partners[stage]
+        return remote(
+            proj_ref if from_input else place,
+            place,
+            c_send.at[stage, index],
+            c_recv.at[stage, index],
+            part,
+            other,
+        )
+
+    def proj_source(index, of_device, of_part):
+        device = of_device
+        if index & 1:
+            device = flip(device, peers // 2)
+        if index & 2:
+            device = flip(device, peers // 4)
+        if index & 4:
+            device = flip(device, 2)
+        return (1 - of_part if index & 8 else of_part), device
+
+    def proj_forward(index):
+        first = index.bit_length()
+        part, device = proj_source(index, me, plane)
+        for stage in range(first, 5):
+            start(proj_copy(stage, index, part, device, from_input=index == 0))
+
+    def proj_wait(index):
+        stage = index.bit_length() - 1
+        part, device = proj_source(index, me, plane)
+        proj_copy(stage, index - (1 << stage), part, device).wait_recv()
+
+    def proj_serve(index):
+        proj_wait(index)
+        proj_forward(index)
+
+    proj_forward(0)
+
+    def block_copies(target, source_places):
+        return (
+            (q_stage.at[target], q_in.at[source_places]),
+            (mix_stage.at[target + 1], mix_in.at[source_places]),
+            (nope_ref.at[:, :, own_columns(target * head)], nope_in.at[source_places]),
+            (value_ref.at[:, :, own_columns(target * head)], value_in.at[source_places]),
+        )
+
+    def a_copy(offset, which):
+        target = (me + offset) % peers
+        src, dst = block_copies(target, own_places(me))[which]
+        return remote(
+            src, dst, a_send.at[offset, which], a_recv.at[offset, which], plane, target
+        )
+
+    order = sorted(range(1, peers), key=lambda offset: (abs(offset - peers // 2), offset))
+    for offset in order[:3]:
+        for which in (2, 3):
+            start(a_copy(offset, which))
+
+    load_q.wait()
+    load_rope.wait()
+    lane = lax.broadcasted_iota(jnp.int32, (block * streams, head), 1)
+    low = lane < ROPE
+
+    def wide(x):
+        return x.astype(jnp.float32)
+
+    def turn(x):
+        return pltpu.roll(x, ROPE, 1)
+
+    rope_low = wide(mix_stage[0].reshape(block * streams, head))
+    rope_high = turn(rope_low)
+    for pair in range(HEADS // 2):
+        first = pair * 3 * head
+        one, two, three = (
+            q_own[:, :, first + i * head : first + (i + 1) * head].reshape(block * streams, head)
+            for i in range(3)
+        )
+        two, three = wide(two), wide(three)
+        shape = (block, streams, head)
+
+        def narrow(x):
+            return x.astype(jnp.bfloat16).reshape(shape)
+
+        q_stage[2 * pair] = one.reshape(shape)
+        mix_stage[2 * pair + 1] = narrow(jnp.where(low, two, rope_high))
+        q_stage[2 * pair + 1] = narrow(turn(jnp.where(low, three, two)))
+        mix_stage[2 * pair + 2] = narrow(jnp.where(low, rope_low, three))
+    for offset in order[:3]:
+        for which in (0, 1):
+            start(a_copy(offset, which))
+    own = [
+        pltpu.make_async_copy(src, dst, load_sem.at[3 + i])
+        for i, (src, dst) in enumerate(block_copies(me, own_places(me)))
+    ]
+    for copy in own:
+        copy.start()
+    proj_serve(1)
+    for offset in order[3:]:
+        for which in range(4):
+            start(a_copy(offset, which))
+
+    odd = jnp.full((block, head), me % 2, jnp.int32)
+    here = lax.broadcasted_iota(jnp.int32, (block, head), 1) // ROPE
+    kept = here == odd
+
+    def unpack(device):
+        places = own_places(device)
+        for stream in range(streams):
+            mix = wide(mix_in[places, stream, :])
+            q_all[stream, places, :head] = q_in[places, stream, :]
+            q_all[stream, places, head:] = jnp.where(kept, mix, 0.0).astype(jnp.bfloat16)
+            key_all[stream, places, :head] = nope_in[places, stream, :]
+            key_all[stream, places, head:] = jnp.where(kept, turn(mix), 0.0).astype(
+                jnp.bfloat16
+            )
+            value_all[stream, places, :] = value_in[places, stream, :]
+
+    for copy in own:
+        copy.wait()
+    unpack(me)
+    proj_serve(2)
+    proj_serve(3)
+    served = 4
+    for offset in order:
+        source = (me + peers - offset) % peers
+        for which in range(4):
+            src, dst = block_copies(source, own_places(source))[which]
+            remote(
+                src, dst, a_send.at[offset, which], a_recv.at[offset, which], plane, source
+            ).wait_recv()
+        unpack(source)
+        if served < 8:
+            proj_serve(served)
+            served += 1
+    while served < 12:
+        proj_serve(served)
+        served += 1
+
+    scale = (NOPE + ROPE) ** (-0.5) * 1.4426950408889634
+    query_rows = length // 4
+    group = query_rows // block
+    begins = [
+        jnp.sum(1 - segments_ref[stream : stream + 1, :], axis=1, keepdims=True)
+        for stream in range(streams)
+    ]
+    spot_row = lax.broadcasted_iota(jnp.int32, (block * streams, block * streams), 0)
+    spot_column = lax.broadcasted_iota(jnp.int32, (block * streams, block * streams), 1)
+    weave = jnp.where(
+        spot_column == (spot_row % streams) * block + spot_row // streams, 1.0, 0.0
+    ).astype(jnp.bfloat16)
+
+    def b_copy(target):
+        return remote(
+            out_stage.at[target],
+            attn.at[:, own_columns(me * head)],
+            b_send.at[target],
+            b_recv.at[me],
+            plane,
+            target,
+        )
+
+    for part in range(3, -1, -1):
+        rows = pl.ds(part * query_rows, query_rows)
+        seen = (part + 1) * query_rows
+        outs = []
+        for stream in range(streams):
+            scores = lax.dot_general(
+                q_all[stream, rows, :],
+                key_all[stream, :seen, :],
+                (((1,), (1,)), ((), ())),
+                preferred_element_type=jnp.float32,
+            )
+            row_at = part * query_rows + lax.broadcasted_iota(jnp.int32, (query_rows, 1), 0)
+            column_at = lax.broadcasted_iota(jnp.int32, (query_rows, seen), 1)
+            first_key = jnp.where(row_at >= begins[stream], begins[stream], 0)
+            allowed = (column_at <= row_at) & (column_at >= first_key)
+            scores = jnp.where(allowed, scores, -jnp.inf)
+            peak = jnp.max(scores, axis=1, keepdims=True)
+            raised = jnp.exp2((scores - peak) * scale)
+            total = jnp.sum(raised, axis=1, keepdims=True)
+            mixed = jnp.dot(
+                raised.astype(jnp.bfloat16),
+                value_all[stream, :seen, :],
+                preferred_element_type=jnp.float32,
+            )
+            outs.append((mixed / total).astype(jnp.bfloat16))
+        for at in range(group):
+            target = part * group + at
+            both = jnp.concatenate(
+                [out[at * block : (at + 1) * block, :] for out in outs], axis=0
+            )
+            out_stage[target] = jnp.dot(
+                weave, both, preferred_element_type=jnp.float32
+            ).astype(jnp.bfloat16)
+
+            @pl.when(me != target)
+            def _():
+                b_copy(target).start()
+
+            @pl.when(me == target)
+            def _():
+                pltpu.make_async_copy(
+                    out_stage.at[target], attn.at[:, own_columns(me * head)], load_sem.at[7]
+                ).start()
+
+    while served < 16:
+        proj_wait(served)
+        start(
+            proj_copy(4, served, *proj_source(served, me, plane))
+        )
+        served += 1
+    load_proj.wait()
+    for index in range(16):
+        part, device = proj_source(index, mate, plane)
+        proj_copy(4, index, part, device).wait_recv()
+
+    for offset in order:
+        source = (me + peers - offset) % peers
+        remote(
+            out_stage.at[source],
+            attn.at[:, own_columns(source * head)],
+            b_send.at[source],
+            b_recv.at[source],
+            plane,
+            source,
+        ).wait_recv()
+    pltpu.make_async_copy(
+        out_stage.at[me], attn.at[:, own_columns(me * head)], load_sem.at[7]
+    ).wait()
+
+    squares = jnp.zeros((block * streams, 1), jnp.float32)
+    step = 4 * head
+    for first in range(0, width, step):
+        projected = jnp.dot(
+            attn[...], proj[:, first : first + step], preferred_element_type=jnp.float32
+        )
+        before = jnp.concatenate(
+            [
+                residual_ref[:, :, at : at + head].reshape(block * streams, head)
+                for at in range(first, first + step, head)
+            ],
+            axis=1,
+        )
+        hidden = before.astype(jnp.float32) + projected
+        hidden_ref[:, first : first + step] = hidden
+        squares = squares + jnp.sum(hidden * hidden, axis=1, keepdims=True)
+    factor = lax.rsqrt(squares * (1.0 / width) + EPSILON)
+    for first in range(0, width, step):
+        gain = gain_ref[:, first : first + step].astype(jnp.float32)
+        normed_ref[:, first : first + step] = (
+            hidden_ref[:, first : first + step] * factor * gain
+        ).astype(jnp.bfloat16)
+
+    for copy in sent:
+        copy.wait_send()
+    for target in range(peers):
+
+        @pl.when(me != target)
+        def _():
+            b_copy(target).wait_send()
+
+
+def attend_and_project(
+    queries, key_nope, key_rope, values, residual, segments, out_proj, norm_gain, peers
+):
+    block, streams, q_width = queries.shape
+    width = residual.shape[2]
+    tokens = block * streams
+    length = block * peers
+    vmem = pl.BlockSpec(memory_space=pltpu.VMEM)
+    anywhere = pl.BlockSpec(memory_space=pl.ANY)
+    dma = pltpu.SemaphoreType.DMA
+    arrived = pltpu.VMEM((length, streams, NOPE), jnp.bfloat16)
+    rope = jnp.pad(key_rope, ((0, 0), (0, 0), (0, NOPE - ROPE)))
+    return pl.pallas_call(
+        functools.partial(attention_kernel, peers),
+        out_shape=(
+            jax.ShapeDtypeStruct((tokens, width), jnp.float32),
+            jax.ShapeDtypeStruct((tokens, width), jnp.bfloat16),
+        ),
+        in_specs=[anywhere, anywhere, anywhere, anywhere, vmem, vmem, anywhere, vmem],
+        out_specs=(vmem, vmem),
+        scratch_shapes=[
+            pltpu.VMEM((block, streams, q_width), jnp.bfloat16),
+            pltpu.VMEM((peers, block, streams, NOPE), jnp.bfloat16),
+            pltpu.VMEM((peers + 1, block, streams, NOPE), jnp.bfloat16),
+            arrived,
+            arrived,
+            arrived,
+            arrived,
+            pltpu.VMEM((streams, length, 2 * NOPE), jnp.bfloat16),
+            pltpu.VMEM((streams, length, 2 * NOPE), jnp.bfloat16),
+            pltpu.VMEM((streams, length, V_DIM), jnp.bfloat16),
+            pltpu.VMEM((peers, tokens, V_DIM), jnp.bfloat16),
+            pltpu.VMEM((tokens, HEADS * V_DIM), jnp.bfloat16),
+            pltpu.VMEM((HEADS * V_DIM, width), jnp.bfloat16),
+            dma((8,)),
+            dma((peers, 4)),
+            dma((peers, 4)),
+            dma((peers,)),
+            dma((peers,)),
+            dma((5, 16)),
+            dma((5, 16)),
+        ],
+        compiler_params=pltpu.CompilerParams(
+            collective_id=0, has_side_effects=True, vmem_limit_bytes=64000000
+        ),
+    )(
+        queries,
+        key_nope,
+        rope,
+        values,
+        residual,
+        segments,
+        out_proj,
+        norm_gain.reshape(1, width),
+    )
+
+
 def attend_items(query_items, key_items, value_items, segment_items):
     length, count_items, qk_width = query_items.shape
     block_rows = QUERY_BLOCK
@@ -349,6 +772,53 @@
 
     blocks = lax.map(one_block, jnp.arange(length // block_rows, dtype=jnp.int32))
     return blocks.reshape(length, count_items, value_items.shape[2])
+
+
+def attend_by_heads(
+    queries, key_nope, key_rope, values, residual, segments, out_proj, norm_gain, expert_count
+):
+    half_rows, stream_count, query_width = queries.shape
+    model_width = residual.shape[2]
+    token_rows = half_rows * stream_count
+    item_count = stream_count * HEADS // expert_count
+    key_heads = jnp.concatenate(
+        [
+            key_nope.reshape(half_rows, stream_count, HEADS, NOPE),
+            jnp.broadcast_to(key_rope[:, :, None, :], (half_rows, stream_count, HEADS, ROPE)),
+        ],
+        axis=3,
+    )
+    query_items = queries.reshape(half_rows, stream_count * HEADS, NOPE + ROPE)
+    key_items = key_heads.reshape(half_rows, stream_count * HEADS, NOPE + ROPE)
+    value_items = values.reshape(half_rows, stream_count * HEADS, V_DIM)
+    packed = jnp.concatenate([query_items, key_items, value_items], axis=2)
+    packed_all = lax.all_to_all(packed, "expert", split_axis=1, concat_axis=0, tiled=True)
+    qk_width = NOPE + ROPE
+    query_all = packed_all[:, :, :qk_width]
+    key_all = packed_all[:, :, qk_width : 2 * qk_width]
+    value_all = packed_all[:, :, 2 * qk_width :]
+    item_ids = lax.axis_index("expert") * item_count + jnp.arange(item_count, dtype=jnp.int32)
+    stream_ids = item_ids // HEADS
+    selector = (stream_ids[:, None] == jnp.arange(stream_count, dtype=jnp.int32)[None, :]).astype(
+        jnp.int32
+    )
+    segment_items = jnp.sum(selector[:, :, None] * segments[None, :, :], axis=1)
+    attended_items = attend_items(query_all, key_all, value_all, segment_items)
+    attended_back = lax.all_to_all(
+        attended_items, "expert", split_axis=0, concat_axis=1, tiled=True
+    )
+    attn_rows = attended_back.reshape(token_rows, HEADS * V_DIM)
+    projected = jnp.dot(
+        attn_rows,
+        lax.all_gather(out_proj, ("dp", "expert"), axis=0, tiled=True),
+        preferred_element_type=jnp.float32,
+    )
+    hidden = residual.reshape(token_rows, model_width).astype(jnp.float32) + projected
+    mean_square = jnp.mean(hidden * hidden, axis=1, keepdims=True)
+    normed = (hidden * lax.rsqrt(mean_square + EPSILON) * norm_gain.astype(jnp.float32)).astype(
+        jnp.bfloat16
+    )
+    return hidden, normed
 
 
 def body(
@@ -370,43 +840,11 @@
     model_width = residual.shape[2]
     token_rows = half_rows * stream_count
     expert_count = lax.axis_size("expert")
-    item_count = stream_count * HEADS // expert_count
-    key_heads = jnp.concatenate(
-        [
-            key_nope.reshape(half_rows, stream_count, HEADS, NOPE),
-            jnp.broadcast_to(key_rope[:, :, None, :], (half_rows, stream_count, HEADS, ROPE)),
-        ],
-        axis=3,
-    )
-    query_items = queries.reshape(half_rows, stream_count * HEADS, NOPE + ROPE)
-    key_items = key_heads.reshape(half_rows, stream_count * HEADS, NOPE + ROPE)
-    value_items = values.reshape(half_rows, stream_count * HEADS, V_DIM)
-    packed = jnp.concatenate([query_items, key_items, value_items], axis=2)
-    packed_all = lax.all_to_all(packed, "expert", split_axis=1, concat_axis=0, tiled=True)
-    qk_width = NOPE + ROPE
-    query_all = packed_all[:, :, :qk_width]
-    key_all = packed_all[:, :, qk_width : 2 * qk_width]
-    value_all = packed_all[:, :, 2 * qk_width :]
-    item_ids = lax.axis_index("expert") * item_count + jnp.arange(item_count, dtype=jnp.int32)
-    stream_ids = item_ids // HEADS
-    selector = (stream_ids[:, None] == jnp.arange(stream_count, dtype=jnp.int32)[None, :]).astype(
-        jnp.int32
-    )
-    segment_items = jnp.sum(selector[:, :, None] * segments[None, :, :], axis=1)
-    attended_items = attend_items(query_all, key_all, value_all, segment_items)
-    attended_back = lax.all_to_all(
-        attended_items, "expert", split_axis=0, concat_axis=1, tiled=True
-    )
-    attn_rows = attended_back.reshape(token_rows, HEADS * V_DIM)
-    projected = jnp.dot(
-        attn_rows,
-        lax.all_gather(out_proj, ("dp", "expert"), axis=0, tiled=True),
-        preferred_element_type=jnp.float32,
-    )
-    hidden = residual.reshape(token_rows, model_width).astype(jnp.float32) + projected
-    mean_square = jnp.mean(hidden * hidden, axis=1, keepdims=True)
-    normed = (hidden * lax.rsqrt(mean_square + EPSILON) * norm_gain.astype(jnp.float32)).astype(
-        jnp.bfloat16
+    attend = attend_by_heads
+    if expert_count == HEADS and lax.axis_size("dp") == 2 and stream_count == 2:
+        attend = attend_and_project
+    hidden, normed = attend(
+        queries, key_nope, key_rope, values, residual, segments, out_proj, norm_gain, expert_count
     )
     token_routes = routes.reshape(token_rows, TOP)
     token_weights = route_weights.reshape(token_rows, TOP)

time: 238 us -> 193 us (0.81)
  Pallas kernels: 96.5 us -> 186 us
  waiting for transfers between devices: 69.9 us -> 0 us
  starting transfers between devices: 18.7 us -> 0 us
  matrix products: 16.1 us -> 0 us
  between operations: 13.6 us -> 0.02 us
  local copies, waits for them, and re-layouts: 17.4 us -> 6.24 us
  other arithmetic: 3.51 us -> 0.61 us
    pallas_call x0 -> x1, Pallas kernels: none -> 90 us  [attend_and_project(): pl.pallas_call(functools.partial(attention_kernel, peers), out_shape=(jax...]
    all_to_all x2 -> x0, waiting for transfers between devices: 69.2 us -> none  [the longest x1 56 us: body(): lax.all_to_all(packed, 'expert', split_axis=1, concat_axis=0, tiled=True)]
    all_to_all x2 -> x0, starting transfers between devices: 18.7 us -> none  [the longest x1 11.2 us: body(): lax.all_to_all(attended_items, 'expert', split_axis=0, concat_axis=1, til...]
    dot_general x3 -> x0, matrix products: 11.8 us -> none  [the longest x2 7.09 us: one_block(): jnp.einsum('iqk,kid->qid', weights, value_items, preferred_element_type=j...]
    reshape x4 -> x1, local copies, waits for them, and re-layouts: 6.79 us -> 1.29 us  [attend_and_project(): norm_gain.reshape(1, width)]
    sub x2 -> x0, matrix products: 4.23 us -> none  [one_block(): raised = jnp.exp(scores - row_peak)]
    concatenate x2 -> x0, local copies, waits for them, and re-layouts: 3.93 us -> none  [the longest x1 2.55 us: body(): packed = jnp.concatenate([query_items, key_items, value_items], axis=2)]
  transfers between devices with their start and end apart: 3 -> 0, of which waited for: 2 -> 0; matrix products, arithmetic and copies ran while one was open for 12% -> 0% of each run, Pallas kernels for 0% -> 0%
where the time goes in v2:
time: 193 us
  Pallas kernels  186 us (96%)
  local copies, waits for them, and re-layouts  6.24 us (3%)
    pallas_call x1, Pallas kernels, routed_experts(): pl.pallas_call(functools.partial(expert_kernel, chips), out_shape=jax.Sha...  96 us
    pallas_call x1, Pallas kernels, attend_and_project(): pl.pallas_call(functools.partial(attention_kernel, peers), out_shape=(jax...  90 us

profile of v2, /device:TPU:0, one launch (start us, length us, event | category | flops | bytes accessed | tf_op | source)
XLA Modules:
  0.0 192.8 jit_solution(13064350606431753720)
XLA Ops:
  0.0 0.7 copy.21
  0.7 0.7 copy.20
  1.4 0.6 select_reduce_fusion
  2.0 1.3 reshape.8.gain_ref
  3.3 1.4 pad.4.rope_ref
  4.7 90.0 %shard_map.127 = (f32[128,2048]{1,0:T(8,128)}, bf16[128,2048]{1,0:T(8,128)(2,1)}) custom-call(bf16[64,2,3072]{2,1,0:T(2,128)(2,1)} %q_ref.1, bf16[64,2,2048]{2,1,0:T(2,128)(2,1)} %nope_ref.1, bf16[64,2,128]{2,1,0:T(2,128)(2,1)} %pad.4.rope_ref, bf16[64,2,2048]{2,1,0:T(2,128)(2,1)} %value_ref.1, bf16[64,2,2048]{2,1,0:T(2,128)(2,1)} %residual_ref.1, ...), custom_call_target="tpu_custom_call" | custom-call | tf_op jit(solution)/shard_map/pallas_call | solution.py:702
  94.7 96.0 %shard_map.128 = bf16[128,2048]{1,0:T(8,128)(2,1)} custom-call(bf16[128,2048]{1,0:T(8,128)(2,1)} %get-tuple-element.7.x_ref, f32[16,128]{1,0:T(8,128)} %bitcast.17, f32[128,2048]{1,0:T(8,128)} %get-tuple-element.8.hidden_ref, bf16[704,2048]{1,0:T(8,128)(2,1)} %bitcast.14, bf16[704,2048]{1,0:T(8,128)(2,1)} %bitcast.15, bf16[704,2048]{1,0:T(8,128)(2,1)} %bitcast.16), custom_call_target="tpu_custom_call" | custom-call | tf_op jit(solution)/shard_map/pallas_call | solution.py:293
  190.7 2.2 %reshape.9 = bf16[64,2,2048]{2,1,0:T(2,128)(2,1)} reshape(bf16[128,2048]{1,0:T(8,128)(2,1)} %shard_map.128) | data formatting | bytes 1048576 | tf_op jit(solution)/shard_map/reshape | solution.py:866

commit v3 on v2

--- a/solution.py
+++ b/solution.py
@@ -31,15 +31,16 @@
     return (1 - back) * (2 * position) + back * (2 * (chips - 1 - position) + 1)
 
 
-def expert_kernel(
+def expert_part(
     chips,
+    alone,
+    store,
     x_ref,
     table_ref,
     hidden_ref,
     gate_ref,
     up_ref,
     down_ref,
-    out_ref,
     rows_all,
     table_all,
     own_part,
@@ -80,9 +81,10 @@
 
     targets = (after, before)
 
-    barrier = pltpu.get_barrier_semaphore()
-    for other in (after, before, mate):
-        pl.semaphore_signal(barrier, inc=1, device_id={"expert": other}, device_id_type=MESH)
+    if alone:
+        barrier = pltpu.get_barrier_semaphore()
+        for other in (after, before, mate):
+            pl.semaphore_signal(barrier, inc=1, device_id={"expert": other}, device_id_type=MESH)
 
     loads = [
         pltpu.make_async_copy(src, dst, weight_sem.at[i])
@@ -92,7 +94,9 @@
     ]
     for load in loads:
         load.start()
-    pl.semaphore_wait(barrier, 3)
+    if alone:
+        pl.semaphore_wait(barrier, 3)
+    yield
 
     def remote(src, dst, send, recv, other):
         return pltpu.make_async_remote_copy(
@@ -275,46 +279,62 @@
         for way in range(2):
             sum_copy(way, 1, part).wait_recv()
             total = total + ring_in[way, 0, part].astype(jnp.float32)
-        out_ref[rows_of(part), :] = total.astype(jnp.bfloat16)
+        store(part * half, total.astype(jnp.bfloat16))
     for copy in sent:
         copy.wait_send()
-
+    yield
+
+
+def expert_kernel(chips, x_ref, table_ref, hidden_ref, gate_ref, up_ref, down_ref, out_ref, *scratch):
+    def store(first, rows):
+        out_ref[pl.ds(first, rows.shape[0]), :] = rows
+
+    part = expert_part(
+        chips, True, store, x_ref, table_ref, hidden_ref, gate_ref, up_ref, down_ref, *scratch
+    )
+    next(part)
+    next(part)
+
+
+def expert_scratch(tokens, width, count, units):
+    chips = count // 2
+    half = tokens // 2
+    far = chips // 2
+    dma = pltpu.SemaphoreType.DMA
+    return [
+        pltpu.VMEM((chips, 2, tokens, width), jnp.bfloat16),
+        pltpu.VMEM((chips, 2, count, tokens), jnp.float32),
+        pltpu.VMEM((chips, tokens, width), jnp.bfloat16),
+        pltpu.VMEM((chips, tokens, width), jnp.bfloat16),
+        pltpu.VMEM((2, far, 2, half, width), jnp.bfloat16),
+        pltpu.VMEM((2 * tokens, units), jnp.bfloat16),
+        pltpu.VMEM((units, width), jnp.bfloat16),
+        pltpu.VMEM((units, width), jnp.bfloat16),
+        pltpu.VMEM((units, width), jnp.bfloat16),
+        dma((3,)),
+        dma((3, chips, 2)),
+        dma((3, chips, 2)),
+        dma((3, chips)),
+        dma((3, chips)),
+        dma((chips,)),
+        dma((chips,)),
+        dma((2, far + 1, 2)),
+        dma((2, far + 1, 2)),
+    ]
 
 def routed_experts(normed, table, hidden, gate, up, down):
     tokens, width = normed.shape
     count = table.shape[0]
     chips = count // 2
     units = gate.shape[0]
-    half = tokens // 2
     vmem = pl.BlockSpec(memory_space=pltpu.VMEM)
     anywhere = pl.BlockSpec(memory_space=pl.ANY)
-    dma = pltpu.SemaphoreType.DMA
-    far = chips // 2
     return pl.pallas_call(
         functools.partial(expert_kernel, chips),
         out_shape=jax.ShapeDtypeStruct((tokens, width), jnp.bfloat16),
         in_specs=[vmem, vmem, vmem, anywhere, anywhere, anywhere],
         out_specs=vmem,
-        scratch_shapes=[
-            pltpu.VMEM((chips, 2, tokens, width), jnp.bfloat16),
-            pltpu.VMEM((chips, 2, count, tokens), jnp.float32),
-            pltpu.VMEM((chips, tokens, width), jnp.bfloat16),
-            pltpu.VMEM((chips, tokens, width), jnp.bfloat16),
-            pltpu.VMEM((2, far, 2, half, width), jnp.bfloat16),
-            pltpu.VMEM((2 * tokens, units), jnp.bfloat16),
-            pltpu.VMEM((units, width), jnp.bfloat16),
-            pltpu.VMEM((units, width), jnp.bfloat16),
-            pltpu.VMEM((units, width), jnp.bfloat16),
-            dma((3,)),
-            dma((3, chips, 2)),
-            dma((3, chips, 2)),
-            dma((3, chips)),
-            dma((3, chips)),
-            dma((chips,)),
-            dma((chips,)),
-            dma((2, far + 1, 2)),
-            dma((2, far + 1, 2)),
-        ],
+        scratch_shapes=expert_scratch(tokens, width, count, units),
         compiler_params=pltpu.CompilerParams(
             collective_id=1, has_side_effects=True, vmem_limit_bytes=64000000
         ),
@@ -325,7 +345,7 @@
     return device + bit - 2 * bit * ((device // bit) % 2)
 
 
-def attention_kernel(
+def attention_part(
     peers,
     q_ref,
     nope_ref,
@@ -338,12 +358,9 @@
     hidden_ref,
     normed_ref,
     q_own,
-    q_stage,
-    mix_stage,
-    q_in,
-    mix_in,
-    nope_in,
-    value_in,
+    rope_own,
+    stage,
+    arrived,
     q_all,
     key_all,
     value_all,
@@ -351,6 +368,7 @@
     attn,
     proj,
     load_sem,
+    stage_sem,
     a_send,
     a_recv,
     b_send,
@@ -380,9 +398,6 @@
         barrier, inc=1, device_id={"dp": 1 - plane, "expert": me}, device_id_type=MESH
     )
 
-    def own_columns(first):
-        return pl.ds(pl.multiple_of(first, head), head)
-
     def own_places(device):
         return pl.ds(pl.multiple_of(device * block, block), block)
 
@@ -392,11 +407,20 @@
         )
 
     load_q = pltpu.make_async_copy(q_ref, q_own, load_sem.at[0])
-    load_rope = pltpu.make_async_copy(rope_ref, mix_stage.at[0], load_sem.at[1])
+    load_rope = pltpu.make_async_copy(rope_ref, rope_own, load_sem.at[1])
     load_proj = pltpu.make_async_copy(
         proj_ref, proj.at[proj_place(plane, me)], load_sem.at[2]
     )
-    for load in (load_q, load_rope, load_proj):
+    staged = [
+        pltpu.make_async_copy(
+            src.at[:, :, target * head : (target + 1) * head],
+            stage.at[target, 2 + i],
+            stage_sem.at[target, i],
+        )
+        for target in range(peers)
+        for i, src in enumerate((nope_ref, value_ref))
+    ]
+    for load in [load_q, load_rope, load_proj] + staged:
         load.start()
     pl.semaphore_wait(barrier, peers)
 
@@ -463,25 +487,17 @@
 
     proj_forward(0)
 
-    def block_copies(target, source_places):
-        return (
-            (q_stage.at[target], q_in.at[source_places]),
-            (mix_stage.at[target + 1], mix_in.at[source_places]),
-            (nope_ref.at[:, :, own_columns(target * head)], nope_in.at[source_places]),
-            (value_ref.at[:, :, own_columns(target * head)], value_in.at[source_places]),
-        )
-
-    def a_copy(offset, which):
-        target = (me + offset) % peers
-        src, dst = block_copies(target, own_places(me))[which]
+    def a_copy(offset, source, target):
         return remote(
-            src, dst, a_send.at[offset, which], a_recv.at[offset, which], plane, target
+            stage.at[target],
+            arrived.at[source],
+            a_send.at[offset],
+            a_recv.at[offset],
+            plane,
+            target if source is me else source,
         )
 
     order = sorted(range(1, peers), key=lambda offset: (abs(offset - peers // 2), offset))
-    for offset in order[:3]:
-        for which in (2, 3):
-            start(a_copy(offset, which))
 
     load_q.wait()
     load_rope.wait()
@@ -494,8 +510,8 @@
     def turn(x):
         return pltpu.roll(x, ROPE, 1)
 
-    rope_low = wide(mix_stage[0].reshape(block * streams, head))
-    rope_high = turn(rope_low)
+    rope_once = wide(rope_own[...]).reshape(block * streams, ROPE)
+    rope_twice = jnp.concatenate([rope_once, rope_once], axis=1)
     for pair in range(HEADS // 2):
         first = pair * 3 * head
         one, two, three = (
@@ -508,60 +524,43 @@
         def narrow(x):
             return x.astype(jnp.bfloat16).reshape(shape)
 
-        q_stage[2 * pair] = one.reshape(shape)
-        mix_stage[2 * pair + 1] = narrow(jnp.where(low, two, rope_high))
-        q_stage[2 * pair + 1] = narrow(turn(jnp.where(low, three, two)))
-        mix_stage[2 * pair + 2] = narrow(jnp.where(low, rope_low, three))
-    for offset in order[:3]:
-        for which in (0, 1):
-            start(a_copy(offset, which))
-    own = [
-        pltpu.make_async_copy(src, dst, load_sem.at[3 + i])
-        for i, (src, dst) in enumerate(block_copies(me, own_places(me)))
-    ]
-    for copy in own:
-        copy.start()
+        stage[2 * pair, 0] = one.reshape(shape)
+        stage[2 * pair, 1] = narrow(jnp.where(low, two, rope_twice))
+        stage[2 * pair + 1, 0] = narrow(turn(jnp.where(low, three, two)))
+        stage[2 * pair + 1, 1] = narrow(jnp.where(low, rope_twice, three))
+    for load in staged:
+        load.wait()
+    for offset in order[:4]:
+        start(a_copy(offset, me, (me + offset) % peers))
     proj_serve(1)
-    for offset in order[3:]:
-        for which in range(4):
-            start(a_copy(offset, which))
+    for offset in order[4:]:
+        start(a_copy(offset, me, (me + offset) % peers))
 
     odd = jnp.full((block, head), me % 2, jnp.int32)
     here = lax.broadcasted_iota(jnp.int32, (block, head), 1) // ROPE
     kept = here == odd
 
-    def unpack(device):
+    def unpack(blocks, device):
         places = own_places(device)
         for stream in range(streams):
-            mix = wide(mix_in[places, stream, :])
-            q_all[stream, places, :head] = q_in[places, stream, :]
+            mix = wide(blocks[device, 1, :, stream, :])
+            q_all[stream, places, :head] = blocks[device, 0, :, stream, :]
             q_all[stream, places, head:] = jnp.where(kept, mix, 0.0).astype(jnp.bfloat16)
-            key_all[stream, places, :head] = nope_in[places, stream, :]
-            key_all[stream, places, head:] = jnp.where(kept, turn(mix), 0.0).astype(
-                jnp.bfloat16
-            )
-            value_all[stream, places, :] = value_in[places, stream, :]
-
-    for copy in own:
-        copy.wait()
-    unpack(me)
+            key_all[stream, places, :head] = blocks[device, 2, :, stream, :]
+            key_all[stream, places, head:] = jnp.where(kept, turn(mix), 0.0).astype(jnp.bfloat16)
+            value_all[stream, places, :] = blocks[device, 3, :, stream, :]
+
+    unpack(stage, me)
     proj_serve(2)
     proj_serve(3)
     served = 4
     for offset in order:
         source = (me + peers - offset) % peers
-        for which in range(4):
-            src, dst = block_copies(source, own_places(source))[which]
-            remote(
-                src, dst, a_send.at[offset, which], a_recv.at[offset, which], plane, source
-            ).wait_recv()
-        unpack(source)
-        if served < 8:
+        a_copy(offset, source, me).wait_recv()
+        unpack(arrived, source)
+        if served < 12:
             proj_serve(served)
             served += 1
-    while served < 12:
-        proj_serve(served)
-        served += 1
 
     scale = (NOPE + ROPE) ** (-0.5) * 1.4426950408889634
     query_rows = length // 4
@@ -579,7 +578,7 @@
     def b_copy(target):
         return remote(
             out_stage.at[target],
-            attn.at[:, own_columns(me * head)],
+            attn.at[me],
             b_send.at[target],
             b_recv.at[me],
             plane,
@@ -626,9 +625,7 @@
 
             @pl.when(me == target)
             def _():
-                pltpu.make_async_copy(
-                    out_stage.at[target], attn.at[:, own_columns(me * head)], load_sem.at[7]
-                ).start()
+                attn[target] = out_stage[target]
 
     while served < 16:
         proj_wait(served)
@@ -645,21 +642,18 @@
         source = (me + peers - offset) % peers
         remote(
             out_stage.at[source],
-            attn.at[:, own_columns(source * head)],
+            attn.at[source],
             b_send.at[source],
             b_recv.at[source],
             plane,
             source,
         ).wait_recv()
-    pltpu.make_async_copy(
-        out_stage.at[me], attn.at[:, own_columns(me * head)], load_sem.at[7]
-    ).wait()
-
+    mixed_rows = jnp.concatenate([attn[at] for at in range(peers)], axis=1)
     squares = jnp.zeros((block * streams, 1), jnp.float32)
     step = 4 * head
     for first in range(0, width, step):
         projected = jnp.dot(
-            attn[...], proj[:, first : first + step], preferred_element_type=jnp.float32
+            mixed_rows, proj[:, first : first + step], preferred_element_type=jnp.float32
         )
         before = jnp.concatenate(
             [
@@ -678,6 +672,7 @@
             hidden_ref[:, first : first + step] * factor * gain
         ).astype(jnp.bfloat16)
 
+    yield
     for copy in sent:
         copy.wait_send()
     for target in range(peers):
@@ -685,10 +680,93 @@
         @pl.when(me != target)
         def _():
             b_copy(target).wait_send()
-
-
-def attend_and_project(
-    queries, key_nope, key_rope, values, residual, segments, out_proj, norm_gain, peers
+    yield
+
+
+def layer_kernel(
+    peers,
+    q_ref,
+    nope_ref,
+    rope_ref,
+    value_ref,
+    residual_ref,
+    segments_ref,
+    proj_ref,
+    gain_ref,
+    routes_ref,
+    weights_ref,
+    gate_ref,
+    up_ref,
+    down_ref,
+    out_ref,
+    hidden,
+    normed,
+    table,
+    *scratch,
+):
+    block, streams, width = out_ref.shape
+    split = 18
+    attention = attention_part(
+        peers,
+        q_ref,
+        nope_ref,
+        rope_ref,
+        value_ref,
+        residual_ref,
+        segments_ref,
+        proj_ref,
+        gain_ref,
+        hidden,
+        normed,
+        *scratch[:split],
+    )
+
+    def store(first, rows):
+        count = rows.shape[0] // streams
+        for at in range(0, width, NOPE):
+            out_ref[pl.ds(first // streams, count), :, at : at + NOPE] = rows[
+                :, at : at + NOPE
+            ].reshape(count, streams, NOPE)
+
+    experts = expert_part(
+        peers // 2,
+        False,
+        store,
+        normed,
+        table,
+        hidden,
+        gate_ref,
+        up_ref,
+        down_ref,
+        *scratch[split:],
+    )
+    choices, tokens = routes_ref.shape[0], routes_ref.shape[2]
+    ids = lax.broadcasted_iota(jnp.int32, (peers, tokens), 0)
+    sums = jnp.zeros((peers, tokens), jnp.float32)
+    for at in range(choices):
+        sums = sums + jnp.where(ids == routes_ref[at], weights_ref[at], 0.0)
+    table[...] = sums
+    next(experts)
+    next(attention)
+    next(experts)
+    next(attention)
+
+
+def whole_layer(
+    queries,
+    key_nope,
+    key_rope,
+    values,
+    residual,
+    segments,
+    out_proj,
+    norm_gain,
+    routes,
+    route_weights,
+    gate,
+    up,
+    down,
+    peers,
 ):
     block, streams, q_width = queries.shape
     width = residual.shape[2]
@@ -697,50 +775,56 @@
     vmem = pl.BlockSpec(memory_space=pltpu.VMEM)
     anywhere = pl.BlockSpec(memory_space=pl.ANY)
     dma = pltpu.SemaphoreType.DMA
-    arrived = pltpu.VMEM((length, streams, NOPE), jnp.bfloat16)
-    rope = jnp.pad(key_rope, ((0, 0), (0, 0), (0, NOPE - ROPE)))
+    blocks = pltpu.VMEM((peers, 4, block, streams, NOPE), jnp.bfloat16)
+    attention_scratch = [
+        pltpu.VMEM((block, streams, q_width), jnp.bfloat16),
+        pltpu.VMEM((block, streams, ROPE), jnp.bfloat16),
+        blocks,
+        blocks,
+        pltpu.VMEM((streams, length, 2 * NOPE), jnp.bfloat16),
+        pltpu.VMEM((streams, length, 2 * NOPE), jnp.bfloat16),
+        pltpu.VMEM((streams, length, V_DIM), jnp.bfloat16),
+        pltpu.VMEM((peers, tokens, V_DIM), jnp.bfloat16),
+        pltpu.VMEM((peers, tokens, V_DIM), jnp.bfloat16),
+        pltpu.VMEM((HEADS * V_DIM, width), jnp.bfloat16),
+        dma((3,)),
+        dma((peers, 2)),
+        dma((peers,)),
+        dma((peers,)),
+        dma((peers,)),
+        dma((peers,)),
+        dma((5, 16)),
+        dma((5, 16)),
+    ]
     return pl.pallas_call(
-        functools.partial(attention_kernel, peers),
-        out_shape=(
-            jax.ShapeDtypeStruct((tokens, width), jnp.float32),
-            jax.ShapeDtypeStruct((tokens, width), jnp.bfloat16),
-        ),
-        in_specs=[anywhere, anywhere, anywhere, anywhere, vmem, vmem, anywhere, vmem],
-        out_specs=(vmem, vmem),
+        functools.partial(layer_kernel, peers),
+        out_shape=jax.ShapeDtypeStruct((block, streams, width), jnp.bfloat16),
+        in_specs=[anywhere] * 4 + [vmem, vmem, anywhere, vmem, vmem, vmem] + [anywhere] * 3,
+        out_specs=vmem,
         scratch_shapes=[
-            pltpu.VMEM((block, streams, q_width), jnp.bfloat16),
-            pltpu.VMEM((peers, block, streams, NOPE), jnp.bfloat16),
-            pltpu.VMEM((peers + 1, block, streams, NOPE), jnp.bfloat16),
-            arrived,
-            arrived,
-            arrived,
-            arrived,
-            pltpu.VMEM((streams, length, 2 * NOPE), jnp.bfloat16),
-            pltpu.VMEM((streams, length, 2 * NOPE), jnp.bfloat16),
-            pltpu.VMEM((streams, length, V_DIM), jnp.bfloat16),
-            pltpu.VMEM((peers, tokens, V_DIM), jnp.bfloat16),
-            pltpu.VMEM((tokens, HEADS * V_DIM), jnp.bfloat16),
-            pltpu.VMEM((HEADS * V_DIM, width), jnp.bfloat16),
-            dma((8,)),
-            dma((peers, 4)),
-            dma((peers, 4)),
-            dma((peers,)),
-            dma((peers,)),
-            dma((5, 16)),
-            dma((5, 16)),
-        ],
+            pltpu.VMEM((tokens, width), jnp.float32),
+            pltpu.VMEM((tokens, width), jnp.bfloat16),
+            pltpu.VMEM((peers, tokens), jnp.float32),
+        ]
+        + attention_scratch
+        + expert_scratch(tokens, width, peers, gate.shape[0]),
         compiler_params=pltpu.CompilerParams(
             collective_id=0, has_side_effects=True, vmem_limit_bytes=64000000
         ),
     )(
         queries,
         key_nope,
-        rope,
+        key_rope,
         values,
         residual,
         segments,
         out_proj,
         norm_gain.reshape(1, width),
+        jnp.transpose(routes, (3, 0, 1, 2)).reshape(-1, 1, tokens),
+        jnp.transpose(route_weights, (3, 0, 1, 2)).reshape(-1, 1, tokens),
+        gate,
+        up,
+        down,
     )
 
 
@@ -840,12 +924,23 @@
     model_width = residual.shape[2]
     token_rows = half_rows * stream_count
     expert_count = lax.axis_size("expert")
-    attend = attend_by_heads
+    gate = jnp.swapaxes(expert_gate[0], 0, 1)
+    up = jnp.swapaxes(expert_up[0], 0, 1)
+    attention_inputs = (
+        queries,
+        key_nope,
+        key_rope,
+        values,
+        residual,
+        segments,
+        out_proj,
+        norm_gain,
+    )
     if expert_count == HEADS and lax.axis_size("dp") == 2 and stream_count == 2:
-        attend = attend_and_project
-    hidden, normed = attend(
-        queries, key_nope, key_rope, values, residual, segments, out_proj, norm_gain, expert_count
-    )
+        return whole_layer(
+            *attention_inputs, routes, route_weights, gate, up, expert_down[0], expert_count
+        )
+    hidden, normed = attend_by_heads(*attention_inputs, expert_count)
     token_routes = routes.reshape(token_rows, TOP)
     token_weights = route_weights.reshape(token_rows, TOP)
     expert_ids = jnp.arange(expert_count, dtype=jnp.int32)
@@ -856,12 +951,7 @@
         axis=1,
     )
     layer_out = routed_experts(
-        normed,
-        weight_table.T,
-        hidden,
-        jnp.swapaxes(expert_gate[0], 0, 1),
-        jnp.swapaxes(expert_up[0], 0, 1),
-        expert_down[0],
+        normed, weight_table.T, hidden, gate, up, expert_down[0]
     )
     return layer_out.reshape(half_rows, stream_count, model_width)
 

time: 193 us -> 182 us (0.943)
  Pallas kernels: 186 us -> 179 us
  local copies, waits for them, and re-layouts: 6.24 us -> 3.49 us
    pallas_call x2 -> x1, Pallas kernels: 186 us -> 179 us  [whole_layer(): pl.pallas_call(functools.partial(layer_kernel, peers), out_shape=jax.Shap...]
    reshape x2 -> x1, local copies, waits for them, and re-layouts: 3.46 us -> 1.29 us  [whole_layer(): norm_gain.reshape(1, width)]
where the time goes in v3:
time: 182 us
  Pallas kernels  179 us (98%)
  local copies, waits for them, and re-layouts  3.49 us (2%)
    pallas_call x1, Pallas kernels, whole_layer(): pl.pallas_call(functools.partial(layer_kernel, peers), out_shape=jax.Shap...  179 us

profile of v3, /device:TPU:0, one launch (start us, length us, event | category | flops | bytes accessed | tf_op | source)
XLA Modules:
  0.0 182.1 jit_solution(104159517768561748)
XLA Ops:
  0.0 1.3 reshape.9.gain_ref
  1.3 178.6 %shard_map.127 = bf16[64,2,2048]{2,1,0:T(2,128)(2,1)} custom-call(bf16[64,2,3072]{2,1,0:T(2,128)(2,1)} %q_ref.1, bf16[64,2,2048]{2,1,0:T(2,128)(2,1)} %nope_ref.1, bf16[64,2,64]{2,1,0:T(2,128)(2,1)} %rope_ref.1, bf16[64,2,2048]{2,1,0:T(2,128)(2,1)} %value_ref.1, bf16[64,2,2048]{2,1,0:T(2,128)(2,1)} %residual_ref.1, s32[2,1024]{1,0:T(2,128)} %segments_ref.1, ...), custom_call_target="tpu_custom_call" | custom-call | tf_op jit(solution)/shard_map/pallas_call | solution.py:799
  179.9 2.2 %copy.17 = bf16[64,2,2048]{2,1,0:T(2,128)(2,1)} copy(bf16[64,2,2048]{2,1,0:T(2,128)(2,1)} %shard_map.127) | data formatting | bytes 1048576

commit v4 on v3

--- a/solution.py
+++ b/solution.py
@@ -15,6 +15,7 @@
 
 
 EPSILON = 1e-06
+FAR_BELOW = -1048576.0
 QUERY_BLOCK = 512
 
 
@@ -175,9 +176,13 @@
                     start(table_copy(way, distance + 1))
                 start(table_copy(2, slot_of(way, distance)))
 
-    def mate_copy(slot):
+    def mate_copy(slot, part):
         return remote(
-            rows_all.at[slot, 1], mate_part.at[slot], m_send.at[slot], m_recv.at[slot], mate
+            rows_all.at[slot, 1, rows_of(part)],
+            mate_part.at[slot, rows_of(part)],
+            m_send.at[slot, part],
+            m_recv.at[slot, part],
+            mate,
         )
 
     hidden_units = gate_vmem.shape[0]
@@ -188,12 +193,25 @@
     def column(row):
         return jnp.sum(jnp.where(eye, row, 0.0), axis=1, keepdims=True)
 
-    def experts(slot):
-        for part in range(2):
+    tabled = {}
+
+    def columns_of(slot):
+        if slot not in tabled:
+            table_copy(2, slot).wait_recv()
+            own_table = table_ref if slot == 0 else table_all.at[slot, 0]
+            tabled[slot] = (
+                column(own_table[pl.ds(me, 1), :]),
+                column(table_all[slot, 1, pl.ds(me, 1), :]),
+            )
+        return tabled[slot]
+
+    def experts(pieces):
+        rows = []
+        for slot, part in pieces:
             row_copy(2, slot, part).wait_recv()
-        table_copy(2, slot).wait_recv()
-        mine = x_ref[...] if slot == 0 else rows_all[slot, 0]
-        rows = jnp.concatenate([mine, rows_all[slot, 1]], axis=0)
+            rows.append(x_ref[rows_of(part), :] if slot == 0 else rows_all[slot, 0, rows_of(part), :])
+            rows.append(rows_all[slot, 1, rows_of(part), :])
+        rows = jnp.concatenate(rows, axis=0)
         for first in range(0, hidden_units, 256):
             count = min(256, hidden_units - first)
             dims = (((1,), (1,)), ((), ()))
@@ -205,18 +223,22 @@
             )
             silu = gate_part / (1.0 + jnp.exp(-gate_part))
             act[:, first : first + count] = (silu * up_part).astype(jnp.bfloat16)
-        own_table = table_ref if slot == 0 else table_all.at[slot, 0]
-        own_column = column(own_table[pl.ds(me, 1), :])
-        mate_column = column(table_all[slot, 1, pl.ds(me, 1), :])
+        scales = [
+            scale[part * half : (part + 1) * half]
+            for slot, part in pieces
+            for scale in columns_of(slot)
+        ]
         for first in range(0, width, 512):
-            y = jnp.dot(
-                act[...], down_vmem[:, first : first + 512], preferred_element_type=jnp.float32
-            )
-            own_part[slot, :, first : first + 512] = (y[:tokens] * own_column).astype(jnp.bfloat16)
-            rows_all[slot, 1, :, first : first + 512] = (y[tokens:] * mate_column).astype(
-                jnp.bfloat16
-            )
-        start(mate_copy(slot))
+            columns = slice(first, first + 512)
+            y = jnp.dot(act[...], down_vmem[:, columns], preferred_element_type=jnp.float32)
+            for at, (slot, part) in enumerate(pieces):
+                for side, place in enumerate((own_part.at[slot], rows_all.at[slot, 1])):
+                    piece = 2 * at + side
+                    place[rows_of(part), columns] = (
+                        y[piece * half : (piece + 1) * half] * scales[piece]
+                    ).astype(jnp.bfloat16)
+        for slot, part in pieces:
+            start(mate_copy(slot, part))
 
     def sum_slot(way, distance):
         return slot_of(1 - way, distance)
@@ -230,15 +252,8 @@
             targets[way],
         )
 
-    mated = set()
-
-    def mated_wait(slot):
-        if slot not in mated:
-            mated.add(slot)
-            mate_copy(slot).wait_recv()
-
     def chip_sum(slot, part):
-        mated_wait(slot)
+        mate_copy(slot, part).wait_recv()
         return own_part[slot, rows_of(part), :].astype(jnp.float32) + mate_part[
             slot, rows_of(part), :
         ].astype(jnp.float32)
@@ -258,17 +273,15 @@
 
     for load in loads:
         load.wait()
-    experts(0)
-    serve(1, 0)
-    serve(1, 1)
+    experts(((0, 0), (0, 1)))
     for distance in range(1, far):
-        experts(slot_of(0, distance))
-        serve(distance + 1, 0)
-        experts(slot_of(1, distance))
-        if distance + 1 < far:
-            serve(distance + 1, 1)
-    send_sum(far - 1, False)
-    experts(slot_of(0, far))
+        for turn in range(2):
+            serve(distance, turn)
+            experts(((slot_of(0, distance), turn), (slot_of(1, distance), 1 - turn)))
+            if distance == far - 1 and turn == 0:
+                send_sum(distance, False)
+    serve(far, 0)
+    experts(((slot_of(0, far), 0), (slot_of(0, far), 1)))
     send_sum(far, True)
     for distance in range(far - 2, 0, -1):
         send_sum(distance, False)
@@ -316,8 +329,8 @@
         dma((3, chips, 2)),
         dma((3, chips)),
         dma((3, chips)),
-        dma((chips,)),
-        dma((chips,)),
+        dma((chips, 2)),
+        dma((chips, 2)),
         dma((2, far + 1, 2)),
         dma((2, far + 1, 2)),
     ]
@@ -497,7 +510,8 @@
             target if source is me else source,
         )
 
-    order = sorted(range(1, peers), key=lambda offset: (abs(offset - peers // 2), offset))
+    order = [(at * 5 + peers // 2) % peers for at in range(peers)]
+    order.remove(0)
 
     load_q.wait()
     load_rope.wait()
@@ -540,14 +554,26 @@
     here = lax.broadcasted_iota(jnp.int32, (block, head), 1) // ROPE
     kept = here == odd
 
+    begins = [
+        jnp.sum(1 - segments_ref[stream : stream + 1, :], axis=1, keepdims=True)
+        for stream in range(streams)
+    ]
+    spare = lax.broadcasted_iota(jnp.int32, (block, head), 1) == ROPE * (1 - odd)
+    place_in = lax.broadcasted_iota(jnp.int32, (block, head), 0)
+
     def unpack(blocks, device):
         places = own_places(device)
         for stream in range(streams):
+            second = place_in + device * block >= begins[stream]
+            q_mark = jnp.where(spare & second, 1.0, 0.0)
+            key_mark = jnp.where(spare & jnp.logical_not(second), FAR_BELOW, 0.0)
             mix = wide(blocks[device, 1, :, stream, :])
             q_all[stream, places, :head] = blocks[device, 0, :, stream, :]
-            q_all[stream, places, head:] = jnp.where(kept, mix, 0.0).astype(jnp.bfloat16)
+            q_all[stream, places, head:] = jnp.where(kept, mix, q_mark).astype(jnp.bfloat16)
             key_all[stream, places, :head] = blocks[device, 2, :, stream, :]
-            key_all[stream, places, head:] = jnp.where(kept, turn(mix), 0.0).astype(jnp.bfloat16)
+            key_all[stream, places, head:] = jnp.where(kept, turn(mix), key_mark).astype(
+                jnp.bfloat16
+            )
             value_all[stream, places, :] = blocks[device, 3, :, stream, :]
 
     unpack(stage, me)
@@ -565,10 +591,6 @@
     scale = (NOPE + ROPE) ** (-0.5) * 1.4426950408889634
     query_rows = length // 4
     group = query_rows // block
-    begins = [
-        jnp.sum(1 - segments_ref[stream : stream + 1, :], axis=1, keepdims=True)
-        for stream in range(streams)
-    ]
     spot_row = lax.broadcasted_iota(jnp.int32, (block * streams, block * streams), 0)
     spot_column = lax.broadcasted_iota(jnp.int32, (block * streams, block * streams), 1)
     weave = jnp.where(
@@ -585,7 +607,10 @@
             target,
         )
 
-    for part in range(3, -1, -1):
+    causal = lax.broadcasted_iota(jnp.int32, (query_rows, query_rows), 1) <= (
+        lax.broadcasted_iota(jnp.int32, (query_rows, query_rows), 0)
+    )
+    for part in (3, 0, 2, 1):
         rows = pl.ds(part * query_rows, query_rows)
         seen = (part + 1) * query_rows
         outs = []
@@ -596,11 +621,11 @@
                 (((1,), (1,)), ((), ())),
                 preferred_element_type=jnp.float32,
             )
-            row_at = part * query_rows + lax.broadcasted_iota(jnp.int32, (query_rows, 1), 0)
-            column_at = lax.broadcasted_iota(jnp.int32, (query_rows, seen), 1)
-            first_key = jnp.where(row_at >= begins[stream], begins[stream], 0)
-            allowed = (column_at <= row_at) & (column_at >= first_key)
-            scores = jnp.where(allowed, scores, -jnp.inf)
+            corner = jnp.where(causal, scores[:, seen - query_rows :], -jnp.inf)
+            if part:
+                scores = jnp.concatenate([scores[:, : seen - query_rows], corner], axis=1)
+            else:
+                scores = corner
             peak = jnp.max(scores, axis=1, keepdims=True)
             raised = jnp.exp2((scores - peak) * scale)
             total = jnp.sum(raised, axis=1, keepdims=True)
@@ -667,7 +692,7 @@
         squares = squares + jnp.sum(hidden * hidden, axis=1, keepdims=True)
     factor = lax.rsqrt(squares * (1.0 / width) + EPSILON)
     for first in range(0, width, step):
-        gain = gain_ref[:, first : first + step].astype(jnp.float32)
+        gain = gain_ref[first : first + step].astype(jnp.float32).reshape(1, step)
         normed_ref[:, first : first + step] = (
             hidden_ref[:, first : first + step] * factor * gain
         ).astype(jnp.bfloat16)
@@ -796,7 +821,7 @@
         dma((5, 16)),
         dma((5, 16)),
     ]
-    return pl.pallas_call(
+    layer_out = pl.pallas_call(
         functools.partial(layer_kernel, peers),
         out_shape=jax.ShapeDtypeStruct((block, streams, width), jnp.bfloat16),
         in_specs=[anywhere] * 4 + [vmem, vmem, anywhere, vmem, vmem, vmem] + [anywhere] * 3,
@@ -819,13 +844,26 @@
         residual,
         segments,
         out_proj,
-        norm_gain.reshape(1, width),
+        norm_gain,
         jnp.transpose(routes, (3, 0, 1, 2)).reshape(-1, 1, tokens),
         jnp.transpose(route_weights, (3, 0, 1, 2)).reshape(-1, 1, tokens),
         gate,
         up,
         down,
     )
+    return pl.pallas_call(
+        copy_kernel,
+        out_shape=jax.ShapeDtypeStruct(layer_out.shape, layer_out.dtype),
+        in_specs=[vmem],
+        out_specs=anywhere,
+        scratch_shapes=[dma],
+    )(layer_out)
+
+
+def copy_kernel(x_ref, out_ref, sem):
+    copy = pltpu.make_async_copy(x_ref, out_ref, sem)
+    copy.start()
+    copy.wait()
 
 
 def attend_items(query_items, key_items, value_items, segment_items):

time: 182 us -> 178 us (0.978)
  local copies, waits for them, and re-layouts: 3.49 us -> 0 us
  Pallas kernels: 179 us -> 177 us
    pallas_call x1, Pallas kernels: 179 us -> 176 us  [whole_layer(): pl.pallas_call(functools.partial(layer_kernel, peers), out_shape=jax.Shap...]
    unnamed x1 -> x0, local copies, waits for them, and re-layouts: 2.2 us -> none
    pallas_call x0 -> x1, Pallas kernels: none -> 1.84 us  [whole_layer(): pl.pallas_call(copy_kernel, out_shape=jax.ShapeDtypeStruct(layer_out.shap...]
where the time goes in v4:
time: 178 us
  Pallas kernels  177 us (99%)
    pallas_call x1, Pallas kernels, whole_layer(): pl.pallas_call(functools.partial(layer_kernel, peers), out_shape=jax.Shap...  176 us

profile of v4, /device:TPU:0, one launch (start us, length us, event | category | flops | bytes accessed | tf_op | source)
XLA Modules:
  0.0 177.6 jit_solution(473254425300023468)
XLA Ops:
  0.0 175.6 %shard_map.127.x_ref = bf16[64,2,2048]{2,1,0:T(2,128)(2,1)} custom-call(bf16[64,2,3072]{2,1,0:T(2,128)(2,1)} %q_ref.1, bf16[64,2,2048]{2,1,0:T(2,128)(2,1)} %nope_ref.1, bf16[64,2,64]{2,1,0:T(2,128)(2,1)} %rope_ref.1, bf16[64,2,2048]{2,1,0:T(2,128)(2,1)} %value_ref.1, bf16[64,2,2048]{2,1,0:T(2,128)(2,1)} %residual_ref.1, s32[2,1024]{1,0:T(2,128)} %segments_ref.1, ...), custom_call_target="tpu_custom_call" | custom-call | tf_op jit(solution)/shard_map/pallas_call | solution.py:824
  175.6 1.8 %shard_map.128 = bf16[64,2,2048]{2,1,0:T(2,128)(2,1)} custom-call(bf16[64,2,2048]{2,1,0:T(2,128)(2,1)} %shard_map.127.x_ref), custom_call_target="tpu_custom_call" | custom-call | tf_op jit(solution)/shard_map/pallas_call | solution.py:854
